TPU v7x, 128 devices: a whole 4x4x4 slice. The times are simulated.
128 devices in a mesh: branch: 64 (over y, z, x_hi, core), head: 2 (over x_lo).
Axes of the slice: x: 4 (x_hi: 2, x_lo: 2; x = x_hi * 2 + x_lo), y: 4, z: 4, core: 2. Of those that a mesh axis runs over, the one named last changes fastest.
Arguments:
- queries: bfloat16 [64, 256, 64, 128], P('branch', None, 'head'), may hold values from -8 to 8
- grad_out: bfloat16 [64, 256, 64, 128], P('branch', None, 'head'), may hold values from -6 to 6
- branch_keys: bfloat16 [64, 256, 8, 128], P('branch', None, 'head'), may hold values from -8 to 8
- branch_values: bfloat16 [64, 256, 8, 128], P('branch', None, 'head'), may hold values from -6 to 6
- row_lse: float32 [64, 64, 256], P('branch', 'head'), may hold values from -100 to 100, as said below
- row_delta: float32 [64, 64, 256], P('branch', 'head'), may hold values from -36 to 36
- lengths: int32 [64], P('branch'), may hold values from 128 to 256, as said below
- prompt_keys: bfloat16 [512, 8, 128], P(('branch', 'head')), may hold values from -8 to 8
- prompt_values: bfloat16 [512, 8, 128], P(('branch', 'head')), may hold values from -6 to 6
Outputs:
- query_grads: bfloat16 [64, 256, 64, 128], P('branch', None, 'head')
- branch_dkey: bfloat16 [64, 256, 8, 128], P('branch', None, 'head')
- branch_dvalue: bfloat16 [64, 256, 8, 128], P('branch', None, 'head')
- prompt_dkey: bfloat16 [512, 8, 128], P(('branch', 'head'))
- prompt_dvalue: bfloat16 [512, 8, 128], P(('branch', 'head'))
Inputs may be any that keep to these rules, and one draw needn't show every extreme that they name: row_lse[b, h, i] is the logarithm of the sum of exp(scaling * queries[b, i, h] . K_b[t, group of h]) over all t < 512 + i + 1, whatever the branch's length. `lengths`: some branch has exactly 256 valid positions and some exactly 128.
All inputs are finite; a program needn't handle non-finite values.
Results may differ from a plain program's by a relative error of at most 0.008.
Values may be sent and summed in bfloat16 or wider, within the bound.
A program may use at most 64 MiB of HBM per device.

v0:
```python
import math

import jax
import jax.numpy as jnp
from jax import lax
from jax.sharding import PartitionSpec as P


def sent_together(arrays, axis, split_dim, concat_dim, along):
    both = jnp.concatenate(arrays, axis=along)
    result, at, outs = (
        lax.all_to_all(both, axis, split_axis=split_dim, concat_axis=concat_dim, tiled=True),
        0,
        [],
    )
    for a in arrays:
        outs.append(lax.slice_in_dim(result, at, at + a.shape[along], axis=along))
        at += a.shape[along]
    return tuple(outs)


def side_by_side(arrays, axis, dim, along):
    widths = [a.shape[along] for a in arrays]
    both = jnp.concatenate(arrays, axis=along)
    result = lax.all_gather(both, axis, axis=dim, tiled=True)
    return tuple(jnp.split(result, [sum(widths[:k]) for k in range(1, len(widths))], axis=along))


def in_blocks(value, dim, devices):
    before, after = (value.shape[:dim], value.shape[dim + 1 :])
    return jnp.moveaxis(value.reshape(*before, devices, -1, *after), dim, 0)


def sum_at_owner(value, axis, dim):
    tiles = in_blocks(value, dim, lax.axis_size(axis))
    arrived = lax.all_to_all(tiles, axis, split_axis=0, concat_axis=0, tiled=True)
    return arrived.astype(jnp.float32).sum(axis=0)


def in_one_piece(arrays, axis, dim, along):
    ends, at = ([], 0)
    for a in arrays[:-1]:
        at += a.shape[along]
        ends.append(at)
    both = jnp.concatenate(arrays, axis=along)
    return tuple(jnp.split(sum_at_owner(both, axis, dim), ends, axis=along))


def score_pieces(queries, grad_out, lse_rows, delta_rows, key_rows, value_rows, visible, scaling):
    scores = (
        jnp.einsum("sgrd,kgd->grsk", queries, key_rows, preferred_element_type=jnp.float32)
        * scaling
    )
    weights = jnp.where(visible, jnp.exp(scores - lse_rows[..., None]), 0.0)
    weights_low = weights.astype(jnp.bfloat16)
    weight_grad = jnp.einsum(
        "sgrd,kgd->grsk", grad_out, value_rows, preferred_element_type=jnp.float32
    )
    score_grad = (weights * (weight_grad - delta_rows[..., None])).astype(jnp.bfloat16)
    query_grad = (
        jnp.einsum("grsk,kgd->sgrd", score_grad, key_rows, preferred_element_type=jnp.float32)
        * scaling
    )
    return (query_grad, weights_low, score_grad)


def edge_grads(weights_low, score_grad, queries, grad_out, scaling):
    value_grad = jnp.einsum(
        "grsk,sgrd->kgd", weights_low, grad_out, preferred_element_type=jnp.float32
    )
    key_grad = (
        jnp.einsum("grsk,sgrd->kgd", score_grad, queries, preferred_element_type=jnp.float32)
        * scaling
    )
    return (key_grad, value_grad)


def block_size():
    return 256


def shards(
    queries,
    grad_out,
    branch_keys,
    branch_values,
    row_lse,
    row_delta,
    lengths,
    prompt_keys,
    prompt_values,
):
    seq_len = queries.shape[1]
    head_count = queries.shape[2]
    head_dim = queries.shape[3]
    groups = branch_keys.shape[2]
    group_size = head_count // groups
    scaling = 1.0 / math.sqrt(head_dim)
    query_grouped = queries[0].reshape(seq_len, groups, group_size, head_dim)
    grad_grouped = grad_out[0].reshape(seq_len, groups, group_size, head_dim)
    lse_rows = row_lse[0].reshape(groups, group_size, seq_len)
    delta_rows = row_delta[0].reshape(groups, group_size, seq_len)
    positions = lax.iota(jnp.int32, seq_len)
    live_rows = positions < lengths[0]
    own_keys, own_values = sent_together((prompt_keys, prompt_values), "head", 1, 0, 2)
    cache_keys, cache_values = side_by_side((own_keys, own_values), "branch", 0, 1)
    query_total = jnp.zeros((seq_len, groups, group_size, head_dim), jnp.float32)
    prompt_len = cache_keys.shape[0]
    prompt_block = block_size()
    prompt_visible = live_rows[:, None]
    dkey_parts = []
    dvalue_parts = []
    for offset in range(0, prompt_len, prompt_block):
        query_part, weights_low, score_grad = score_pieces(
            query_grouped,
            grad_grouped,
            lse_rows,
            delta_rows,
            cache_keys[offset : offset + prompt_block],
            cache_values[offset : offset + prompt_block],
            prompt_visible,
            scaling,
        )
        query_total = query_total + query_part
        key_part, value_part = edge_grads(
            weights_low, score_grad, query_grouped, grad_grouped, scaling
        )
        dkey_parts.append(key_part)
        dvalue_parts.append(value_part)
    branch_block = block_size()
    offset = 0
    key_positions = offset + lax.iota(jnp.int32, branch_block)
    visible = live_rows[:, None] & (key_positions[None, :] <= positions[:, None])
    query_part, weights_low, score_grad = score_pieces(
        query_grouped,
        grad_grouped,
        lse_rows,
        delta_rows,
        branch_keys[0, offset : offset + branch_block],
        branch_values[0, offset : offset + branch_block],
        visible,
        scaling,
    )
    key_part, value_part = edge_grads(weights_low, score_grad, query_grouped, grad_grouped, scaling)
    query_total = query_total + query_part
    own_dkey = key_part.astype(jnp.bfloat16)
    own_dvalue = value_part.astype(jnp.bfloat16)
    prompt_dkey_terms = jnp.concatenate(dkey_parts, 0)
    prompt_dvalue_terms = jnp.concatenate(dvalue_parts, 0)
    summed_keys, summed_values = in_one_piece(
        (prompt_dkey_terms.astype(jnp.bfloat16), prompt_dvalue_terms.astype(jnp.bfloat16)),
        "branch",
        0,
        1,
    )
    prompt_dkey, prompt_dvalue = sent_together(
        (summed_keys.astype(jnp.bfloat16), summed_values.astype(jnp.bfloat16)), "head", 0, 1, 2
    )
    query_grads = query_total.reshape(seq_len, head_count, head_dim).astype(jnp.bfloat16)[None]
    branch_dkey = own_dkey[None]
    branch_dvalue = own_dvalue[None]
    return (query_grads, branch_dkey, branch_dvalue, prompt_dkey, prompt_dvalue)


def solution(mesh):
    in_specs = (
        P("branch", None, "head", None),
        P("branch", None, "head", None),
        P("branch", None, "head", None),
        P("branch", None, "head", None),
        P("branch", "head", None),
        P("branch", "head", None),
        P("branch"),
        P(("branch", "head"), None, None),
        P(("branch", "head"), None, None),
    )
    out_specs = (
        P("branch", None, "head", None),
        P("branch", None, "head", None),
        P("branch", None, "head", None),
        P(("branch", "head"), None, None),
        P(("branch", "head"), None, None),
    )
    return jax.shard_map(shards, mesh=mesh, in_specs=in_specs, out_specs=out_specs, check_vma=False)
```

profile of v0, /device:TPU:1, one launch (start us, length us, event | category | flops | bytes accessed | tf_op | source)
XLA Modules:
  0.0 156.2 jit_solution(11121480625824953689)
XLA Ops:
  7.2 0.0 copy-start
  7.2 0.8 copy.126
  8.0 0.7 copy.127
  8.7 0.6 pad_maximum_fusion.1
  9.3 3.3 %all-to-all-start = ((bf16[4,8,256]{2,0,1:T(4,128)(2,1)}), bf16[4,8,256]{2,0,1:T(4,128)(2,1)S(1)}, u32[]{:S(2)}, u32[]{:S(2)}) async-start(bf16[4,8,256]{2,0,1:T(4,128)(2,1)} %pad_maximum_fusion.1), calls=%async_computation | async-start | bytes 32768 | tf_op jit(solution)/shard_map/all_to_all | solution.py:12
  13.3 2.5 %all-to-all-done = bf16[4,8,256]{2,0,1:T(4,128)(2,1)S(1)} async-done(((bf16[4,8,256]{2,0,1:T(4,128)(2,1)}), bf16[4,8,256]{2,0,1:T(4,128)(2,1)S(1)}, u32[]{:S(2)}, u32[]{:S(2)}) %all-to-all-start) | async-done | bytes 16416 | tf_op jit(solution)/shard_map/all_to_all | solution.py:12
  15.9 0.6 pad_maximum_fusion.2
  16.5 0.0 all-gather.2.cloned.1.call-update
  16.5 0.0 copy-start.11
  16.5 3.0 %fusion.70 = f32[4,256,256,8]{2,1,3,0:T(8,128)S(1)} fusion(bf16[256,4,8,128]{3,2,1,0:T(8,128)(2,1)} %bitcast.207, bf16[256,4,128,1]{2,1,0,3:T(4,128)(2,1)} %bitcast.214), kind=kOutput, calls=%fused_computation.60 | convolution fusion | flops 536870912 | bytes 10747904 | tf_op jit(solution)/shard_map/sgrd,kgd->grsk/dot_general | solution.py:51
  19.6 0.0 copy-start.9
  19.6 0.0 copy-start.10
  19.6 2.4 %fusion.58 = bf16[1,256,4,128]{3,1,2,0:T(8,128)(2,1)S(1)} fusion(f32[4,256,256,8]{2,1,3,0:T(8,128)S(1)} %fusion.70, f32[4,8,256]{2,1,0:T(8,128)S(1)} %bitcast.224, pred[256,256]{0,1:T(8,128)(4,1)S(1)} %fusion.77, bf16[256,4,8,128]{3,2,1,0:T(8,128)(2,1)S(1)} %bitcast.204), kind=kOutput, calls=%fused_computation.49 | convolution fusion | flops 545390592 | bytes 10846208 | tf_op jit(solution)/shard_map/grsk,sgrd->kgd/dot_general | solution.py:68
  22.1 4.9 %fusion.1 = bf16[4,8,256,256]{2,3,1,0:T(8,128)(2,1)} fusion(f32[4,256,256,8]{2,1,3,0:T(8,128)S(1)} %fusion.70, f32[4,8,256]{2,1,0:T(8,128)S(1)} %bitcast.221, f32[4,8,256]{2,1,0:T(8,128)S(1)} %bitcast.225, pred[256,256]{0,1:T(8,128)(4,1)S(1)} %fusion.77, bf16[256,4,8,128]{3,2,1,0:T(8,128)(2,1)S(1)} %bitcast.205, bf16[256,4,128,1]{2,1,0,3:T(4,128)(2,1)S(1)} %bitcast.220), kind=kOutput, calls=%fused_computation.2 | convolution fusion | flops 549453824 | bytes 15073280 | tf_op jit(solution)/shard_map/sgrd,kgd->grsk/dot_general | solution.py:56
  27.0 56.1 %all-gather.2.cloned.1.call-done = bf16[512,8,128]{2,0,1:T(8,128)(2,1)} async-done(((bf16[8,8,128]{2,0,1:T(8,128)(2,1)}), bf16[512,8,128]{2,0,1:T(8,128)(2,1)}) %all-gather.2.cloned.1.call-update) | async-done | bytes 1048592 | tf_op jit(solution)/shard_map/all_gather | solution.py:25
  83.0 3.0 %fusion.72 = f32[4,256,256,8]{2,1,3,0:T(8,128)S(1)} fusion(bf16[256,4,8,128]{3,2,1,0:T(8,128)(2,1)} %bitcast.208, bf16[512,8,128]{2,0,1:T(8,128)(2,1)} %all-gather.2.cloned.1.call-done), kind=kOutput, calls=%fused_computation.62 | convolution fusion | flops 536870912 | bytes 10747904 | tf_op jit(solution)/shard_map/sgrd,kgd->grsk/dot_general | solution.py:51
  86.1 2.3 %fusion.55 = bf16[256,4,128]{2,0,1:T(8,128)(2,1)S(1)} fusion(f32[4,256,256,8]{2,1,3,0:T(8,128)S(1)} %fusion.72, f32[4,8,256]{2,1,0:T(8,128)S(1)} %bitcast.226, pred[256]{0:T(512)(128)(4,1)S(1)} %iota_compare_fusion.1, bf16[256,4,8,128]{3,2,1,0:T(8,128)(2,1)S(1)} %bitcast.202), kind=kOutput, calls=%fused_computation.48 | convolution fusion | flops 545390592 | bytes 10780928 | tf_op jit(solution)/shard_map/grsk,sgrd->kgd/dot_general | solution.py:68
  88.5 0.0 copy-start.1
  88.5 3.2 %fusion.5 = bf16[4,8,256,256]{2,3,1,0:T(8,128)(2,1)S(1)} fusion(f32[4,256,256,8]{2,1,3,0:T(8,128)S(1)} %fusion.72, f32[4,8,256]{2,1,0:T(8,128)S(1)} %bitcast.222, f32[4,8,256]{2,1,0:T(8,128)S(1)} %bitcast.227, pred[256]{0:T(512)(128)(4,1)S(1)} %iota_compare_fusion.1, bf16[256,4,8,128]{3,2,1,0:T(8,128)(2,1)S(1)} %bitcast.206, ...), kind=kOutput, calls=%fused_computation.8 | convolution fusion | flops 549453824 | bytes 15008256 | tf_op jit(solution)/shard_map/sgrd,kgd->grsk/dot_general | solution.py:56
  91.7 0.0 copy-done.1
  91.7 0.0 copy-start.2
  91.7 1.4 fusion.49
  93.1 1.4 fusion.74
  94.5 2.3 %fusion.52 = bf16[256,4,128]{2,0,1:T(8,128)(2,1)S(1)} fusion(f32[4,256,256,8]{2,1,3,0:T(8,128)S(1)} %fusion.74, f32[4,8,256]{2,1,0:T(8,128)S(1)} %bitcast.228, pred[256]{0:T(512)(128)(4,1)S(1)} %iota_compare_fusion.1, bf16[256,4,8,128]{3,2,1,0:T(8,128)(2,1)S(1)} %bitcast.203), kind=kOutput, calls=%fused_computation.47 | convolution fusion | flops 545390592 | bytes 10780928 | tf_op jit(solution)/shard_map/grsk,sgrd->kgd/dot_general | solution.py:68
  96.9 3.4 %fusion.9 = bf16[4,8,256,256]{2,3,1,0:T(8,128)(2,1)S(1)} fusion(f32[4,256,256,8]{2,1,3,0:T(8,128)S(1)} %fusion.74, f32[4,8,256]{2,1,0:T(8,128)S(1)} %bitcast.223, f32[4,8,256]{2,1,0:T(8,128)S(1)} %bitcast.229, pred[256]{0:T(512)(128)(4,1)S(1)} %iota_compare_fusion.1, bf16[256,4,8,128]{3,2,1,0:T(8,128)(2,1)S(1)} %bitcast.201, ...), kind=kOutput, calls=%fused_computation.14 | convolution fusion | flops 549453824 | bytes 15008256 | tf_op jit(solution)/shard_map/sgrd,kgd->grsk/dot_general | solution.py:56
  100.3 0.0 copy-start.4
  100.3 1.5 fusion.50
  101.7 0.1 maximum_bitcast_fusion
  101.8 0.5 copy-done.4
  102.3 0.1 pad_maximum_fusion
  102.4 1.3 copy.189
  103.6 8.7 %all-to-all-start.1 = ((bf16[64,8,8,128]{3,1,2,0:T(8,128)(2,1)}), bf16[64,8,8,128]{3,1,2,0:T(8,128)(2,1)S(1)}, u32[]{:S(2)}, u32[]{:S(2)}) async-start(bf16[64,8,8,128]{3,1,2,0:T(8,128)(2,1)} %copy.189), calls=%async_computation.1 | async-start | bytes 2097152 | tf_op jit(solution)/shard_map/all_to_all | solution.py:36
  112.4 4.4 %fusion.51 = bf16[1,256,4,128]{3,1,2,0:T(8,128)(2,1)S(1)} fusion(bf16[4,8,256,256]{2,3,1,0:T(8,128)(2,1)} %fusion.1, bf16[256,4,8,128]{3,2,1,0:T(8,128)(2,1)} %bitcast.209), kind=kOutput, calls=%fused_computation.46 | convolution fusion | flops 537133056 | bytes 6553600 | tf_op jit(solution)/shard_map/grsk,sgrd->kgd/dot_general | solution.py:72
  116.8 0.9 copy.156
  117.7 0.9 copy.157
  118.6 0.0 copy-done.3
  118.7 2.8 %fusion.81 = f32[4,128,8,256]{3,1,2,0:T(8,128)} fusion(bf16[4,8,256,256]{2,3,1,0:T(8,128)(2,1)S(1)} %copy-done.3, bf16[512,8,128]{2,0,1:T(8,128)(2,1)S(1)} %copy-done.8), kind=kOutput, calls=%fused_computation.78 | convolution fusion | flops 536870912 | bytes 8650752 | tf_op jit(solution)/shard_map/grsk,kgd->sgrd/dot_general | solution.py:61
  121.4 0.6 copy-done.5
  122.0 2.7 %fusion.80 = f32[4,128,8,256]{3,1,2,0:T(8,128)} fusion(bf16[4,8,256,256]{2,3,1,0:T(8,128)(2,1)S(1)} %copy-done.5, bf16[512,8,128]{2,0,1:T(8,128)(2,1)S(1)} %copy-done.8), kind=kOutput, calls=%fused_computation.77 | convolution fusion | flops 536870912 | bytes 8650752 | tf_op jit(solution)/shard_map/grsk,kgd->sgrd/dot_general | solution.py:61
  124.8 7.4 %all-to-all-done.1 = bf16[64,8,8,128]{3,1,2,0:T(8,128)(2,1)S(1)} async-done(((bf16[64,8,8,128]{3,1,2,0:T(8,128)(2,1)}), bf16[64,8,8,128]{3,1,2,0:T(8,128)(2,1)S(1)}, u32[]{:S(2)}, u32[]{:S(2)}) %all-to-all-start.1) | async-done | bytes 1048608 | tf_op jit(solution)/shard_map/all_to_all | solution.py:36
  132.2 0.2 reduce
  132.4 0.6 copy.153
  133.0 3.2 %all-to-all-start.2 = ((bf16[8,4,256]{2,1,0:T(4,128)(2,1)}), bf16[8,4,256]{2,1,0:T(4,128)(2,1)S(1)}, u32[]{:S(2)}, u32[]{:S(2)}) async-start(bf16[8,4,256]{2,1,0:T(4,128)(2,1)} %copy.153), calls=%async_computation.2 | async-start | bytes 32768 | tf_op jit(solution)/shard_map/all_to_all | solution.py:12
  136.2 7.4 %fusion.15 = bf16[256,4,8,128]{0,3,2,1:T(8,128)(2,1)} fusion(f32[4,128,8,256]{3,1,2,0:T(8,128)} %fusion.80, f32[4,128,8,256]{3,1,2,0:T(8,128)} %fusion.81, bf16[4,8,256,256]{2,3,1,0:T(8,128)(2,1)} %fusion.1, bf16[256,4,128,1]{2,1,0,3:T(4,128)(2,1)S(1)} %bitcast.215), kind=kOutput, calls=%fused_computation.22 | convolution fusion | flops 542113792 | bytes 14942208 | tf_op jit(solution)/shard_map/grsk,kgd->sgrd/dot_general | solution.py:61
  143.7 4.5 %copy.155 = bf16[1,256,32,128]{3,2,1,0:T(8,128)(2,1)} copy(bf16[1,256,32,128]{1,3,2,0:T(8,128)(2,1)} %bitcast.213) | data formatting | bytes 4194304
  148.1 0.0 all-to-all-done.2
  148.2 0.6 copy.159
  148.8 0.6 copy.158
  (23 shorter events, 0.1 us)
Async XLA Ops:
  7.2 12.4 %copy-start = (bf16[1,256,32,128]{3,2,1,0:T(8,128)(2,1)S(1)}, bf16[1,256,32,128]{3,2,1,0:T(8,128)(2,1)}, u32[]{:S(2)}) copy-start(bf16[1,256,32,128]{3,2,1,0:T(8,128)(2,1)} %param.10) | copy-start | bytes 6291460
  9.3 6.5 %all-to-all-start = ((bf16[4,8,256]{2,0,1:T(4,128)(2,1)}), bf16[4,8,256]{2,0,1:T(4,128)(2,1)S(1)}, u32[]{:S(2)}, u32[]{:S(2)}) async-start(bf16[4,8,256]{2,0,1:T(4,128)(2,1)} %pad_maximum_fusion.1), calls=%async_computation | async-start | bytes 32768 | tf_op jit(solution)/shard_map/all_to_all | solution.py:12
  12.6 70.4 %all-gather.2.cloned.1.call-start = ((), (), s32[]{:S(2)}) async-start(), calls=%async_computation.3 | async-start | bytes 1064960 | tf_op jit(solution)/shard_map/all_gather | solution.py:25
  16.5 3.1 %copy-start.11 = (f32[1,32,256]{2,1,0:T(8,128)S(1)}, f32[1,32,256]{2,1,0:T(8,128)}, u32[]{:S(2)}) copy-start(f32[1,32,256]{2,1,0:T(8,128)} %param.13) | copy-start | bytes 98308
  19.6 2.4 %copy-start.9 = (bf16[1,256,4,128]{3,2,1,0:T(4,128)(2,1)S(1)}, bf16[1,256,4,128]{3,2,1,0:T(4,128)(2,1)}, u32[]{:S(2)}) copy-start(bf16[1,256,4,128]{3,2,1,0:T(4,128)(2,1)} %param.12) | copy-start | bytes 786436
  19.6 2.4 %copy-start.10 = (f32[1,32,256]{2,1,0:T(8,128)S(1)}, f32[1,32,256]{2,1,0:T(8,128)}, u32[]{:S(2)}) copy-start(f32[1,32,256]{2,1,0:T(8,128)} %param.14) | copy-start | bytes 98308
  86.1 2.4 %copy-start.7 = (bf16[512,8,128]{2,0,1:T(8,128)(2,1)S(1)}, bf16[512,8,128]{2,0,1:T(8,128)(2,1)}, u32[]{:S(2)}) copy-start(bf16[512,8,128]{2,0,1:T(8,128)(2,1)} %all-gather.2.cloned.1.call-done) | copy-start | bytes 3145732
  88.5 3.2 %copy-start.1 = (bf16[1,256,32,128]{3,2,1,0:T(8,128)(2,1)S(1)}, bf16[1,256,32,128]{3,2,1,0:T(8,128)(2,1)}, u32[]{:S(2)}) copy-start(bf16[1,256,32,128]{3,2,1,0:T(8,128)(2,1)} %param.9) | copy-start | bytes 6291460
  91.7 2.8 %copy-start.2 = (bf16[4,8,256,256]{2,3,1,0:T(8,128)(2,1)}, bf16[4,8,256,256]{2,3,1,0:T(8,128)(2,1)S(1)}, u32[]{:S(2)}) copy-start(bf16[4,8,256,256]{2,3,1,0:T(8,128)(2,1)S(1)} %fusion.5) | copy-start | bytes 12582916
  100.3 2.0 %copy-start.4 = (bf16[4,8,256,256]{2,3,1,0:T(8,128)(2,1)}, bf16[4,8,256,256]{2,3,1,0:T(8,128)(2,1)S(1)}, u32[]{:S(2)}) copy-start(bf16[4,8,256,256]{2,3,1,0:T(8,128)(2,1)S(1)} %fusion.9) | copy-start | bytes 12582916
  103.6 28.5 %all-to-all-start.1 = ((bf16[64,8,8,128]{3,1,2,0:T(8,128)(2,1)}), bf16[64,8,8,128]{3,1,2,0:T(8,128)(2,1)S(1)}, u32[]{:S(2)}, u32[]{:S(2)}) async-start(bf16[64,8,8,128]{3,1,2,0:T(8,128)(2,1)} %copy.189), calls=%async_computation.1 | async-start | bytes 2097152 | tf_op jit(solution)/shard_map/all_to_all | solution.py:36
  112.4 6.3 %copy-start.3 = (bf16[4,8,256,256]{2,3,1,0:T(8,128)(2,1)S(1)}, bf16[4,8,256,256]{2,3,1,0:T(8,128)(2,1)}, u32[]{:S(2)}) copy-start(bf16[4,8,256,256]{2,3,1,0:T(8,128)(2,1)} %copy-done.2) | copy-start | bytes 12582916
  112.4 6.3 %copy-start.8 = (bf16[512,8,128]{2,0,1:T(8,128)(2,1)S(1)}, bf16[512,8,128]{2,0,1:T(8,128)(2,1)}, u32[]{:S(2)}) copy-start(bf16[512,8,128]{2,0,1:T(8,128)(2,1)} %all-gather.2.cloned.1.call-done) | copy-start | bytes 3145732
  118.7 3.4 %copy-start.5 = (bf16[4,8,256,256]{2,3,1,0:T(8,128)(2,1)S(1)}, bf16[4,8,256,256]{2,3,1,0:T(8,128)(2,1)}, u32[]{:S(2)}) copy-start(bf16[4,8,256,256]{2,3,1,0:T(8,128)(2,1)} %copy-done.4) | copy-start | bytes 12582916
  122.0 14.2 %copy-start.6 = (bf16[1,256,4,128]{3,2,1,0:T(4,128)(2,1)S(1)}, bf16[1,256,4,128]{3,2,1,0:T(4,128)(2,1)}, u32[]{:S(2)}) copy-start(bf16[1,256,4,128]{3,2,1,0:T(4,128)(2,1)} %param.11) | copy-start | bytes 786436
  133.0 15.2 %all-to-all-start.2 = ((bf16[8,4,256]{2,1,0:T(4,128)(2,1)}), bf16[8,4,256]{2,1,0:T(4,128)(2,1)S(1)}, u32[]{:S(2)}, u32[]{:S(2)}) async-start(bf16[8,4,256]{2,1,0:T(4,128)(2,1)} %copy.153), calls=%async_computation.2 | async-start | bytes 32768 | tf_op jit(solution)/shard_map/all_to_all | solution.py:12
Sparse Core Ops, SparseCore 0:
  16.9 66.0 all-gather.1
where the time goes:
time: 157 us; the launch traced here: 156 us
  waiting for transfers between devices  66 us (42%)
  matrix products  46.3 us (29%)
  starting transfers between devices  15.2 us (10%)
  between operations  15 us (10%)
  local copies, waits for them, and re-layouts  12.1 us (8%)
  other arithmetic  1.61 us (1%)
    all_gather x1, waiting for transfers between devices, side_by_side(): result = lax.all_gather(both, axis, axis=dim, tiled=True)  56.1 us
    dot_general x3, matrix products, score_pieces(): jnp.einsum('grsk,kgd->sgrd', score_grad, key_rows, preferred_element_type...  13 us
    dot_general x3, matrix products, score_pieces(): jnp.einsum('sgrd,kgd->grsk', grad_out, value_rows, preferred_element_type...  11.5 us
    unnamed x31, local copies, waits for them, and re-layouts  10.2 us
    all_to_all x1, starting transfers between devices, sum_at_owner(): lax.all_to_all(tiles, axis, split_axis=0, concat_axis=0, tiled=True)  8.71 us
    dot_general x3, matrix products, score_pieces(): jnp.einsum('sgrd,kgd->grsk', queries, key_rows, preferred_element_type=jn...  7.46 us
    all_to_all x1, waiting for transfers between devices, sum_at_owner(): lax.all_to_all(tiles, axis, split_axis=0, concat_axis=0, tiled=True)  7.38 us
    dot_general x3, matrix products, edge_grads(): jnp.einsum('grsk,sgrd->kgd', score_grad, queries, preferred_element_type=...  7.35 us
  transfers between devices with their start and end apart: 4, of which 3 were waited for; matrix products, arithmetic and copies ran while one was open for 22% of the time, Pallas kernels for 0%

commit v1 on v0

v1 whole, which is shorter than its diff:
```python
import math

import jax
import jax.numpy as jnp
from jax import lax
from jax.experimental import pallas as pl
from jax.experimental.pallas import tpu as pltpu
from jax.sharding import PartitionSpec as P

F32 = jnp.float32
BF16 = jnp.bfloat16
LOG2E = math.log2(math.e)
CHUNK = 32
UNROLL = 4


def remote(src, dst, send_sem, recv_sem, branch, head):
    return pltpu.make_async_remote_copy(
        src_ref=src,
        dst_ref=dst,
        send_sem=send_sem,
        recv_sem=recv_sem,
        device_id={"branch": branch, "head": head},
        device_id_type=pl.DeviceIdType.MESH,
    )


def spread(ref, group, pos, heads):
    row = lax.broadcasted_iota(jnp.int32, (heads, 128), 0)
    lane = lax.broadcasted_iota(jnp.int32, (heads, 128), 1)
    step = 128 // heads
    tile = ref[heads * group : heads * group + heads, pos // 128 * 128 : pos // 128 * 128 + 128]
    outs = []
    for k in range(CHUNK // step):
        index = lax.shift_right_logical(lane, 3) + (pos % 128 + step * k)
        picked = jnp.take_along_axis(tile, index, axis=1, mode="promise_in_bounds")
        picked = jnp.where(row == (lane & (heads - 1)), picked, 0.0)
        outs.append(jnp.sum(picked, axis=0, keepdims=True))
    return jnp.concatenate(outs, axis=1)


def kernel(
    seq, groups, heads, prompt, depth, scale,
    length_ref, q_hbm, do_hbm, lse_hbm, delta_hbm, pk_hbm, pv_hbm, bk_hbm, bv_hbm,
    dq_hbm, dbk_hbm, dbv_hbm, dpk_hbm, dpv_hbm,
    q_s, do_s, dq_s, dq_acc, lse_s, delta_s, rows_s, own_s, bin_s, bkv, wide, kv,
    line, line_f, acc, tail_acc, pair, half, half_in, spot, spot_in, owned, owner_out, owner_in, fin, fin_b,
    bout, in_sem, q_sem, out_sem, line_sem, plane_sem, fwd_sem, pair_sem, red_sem, own_sem,
):
    b, h = lax.axis_index("branch"), lax.axis_index("head")
    plane, place = b // 4, (b % 4) * 2 + h
    core = b % 2
    sibling = b + 1 - 2 * core
    chunks = seq // CHUNK
    n = CHUNK * heads
    exp_scale = scale * LOG2E

    def plane_peer(d):
        return (plane + d) % 16 * 4 + b % 4

    def line_peer(d):
        other = (place + d) % 8
        return other, plane * 4 + other // 2, other % 2

    barrier = pltpu.get_barrier_semaphore()
    for d in range(1, 8):
        _, pb, ph = line_peer(d)
        pl.semaphore_signal(barrier, inc=1, device_id={"branch": pb, "head": ph}, device_id_type=pl.DeviceIdType.MESH)
    for d in range(1, 16):
        pl.semaphore_signal(barrier, inc=1, device_id={"branch": plane_peer(d), "head": h}, device_id_type=pl.DeviceIdType.MESH)

    small = [
        pltpu.make_async_copy(src, dst, in_sem.at[i])
        for i, (src, dst) in enumerate(
            (
                (pk_hbm, own_s.at[0]), (pv_hbm, own_s.at[1]), (lse_hbm, lse_s), (delta_hbm, delta_s),
                (bk_hbm, bin_s.at[0]), (bv_hbm, bin_s.at[1]),
            )
        )
    ]
    large = [
        (
            pltpu.make_async_copy(q_hbm.at[:, g], q_s.at[g], q_sem.at[0, g]),
            pltpu.make_async_copy(do_hbm.at[:, g], do_s.at[g], q_sem.at[1, g]),
        )
        for g in range(groups)
    ]
    for copy in small:
        copy.start()
    for pair_of in large:
        for copy in pair_of:
            copy.start()
    small[0].wait()
    small[1].wait()
    pl.semaphore_wait(barrier, 22)

    for d in range(1, 8):
        other, pb, ph = line_peer(d)
        remote(own_s.at[other // 2 % 2], line.at[place], line_sem.at[0], line_sem.at[1], pb, ph).start()
    line[place] = own_s[core]

    for copy in small[2:]:
        copy.wait()
    position = lax.broadcasted_iota(jnp.int32, (groups * heads, seq), 1)
    lse_s[...] = jnp.where(position < length_ref[0], lse_s[...] * LOG2E, 1e30)
    for kind in range(2):
        wide[...] = bin_s[kind].astype(F32)
        for g in range(groups):
            bkv[kind, g] = wide[pl.ds(g, seq, stride=groups), :].astype(BF16)

    def piece(k, v, q, do, lse, delta, mask):
        st = lax.dot_general(k, q, (((1,), (1,)), ((), ())), preferred_element_type=F32)
        p = jnp.exp2(st * exp_scale - lse)
        if mask is not None:
            keep = k.shape[0] - CHUNK
            tail = jnp.where(mask, p[keep:], 0.0)
            p = jnp.concatenate([p[:keep], tail], axis=0) if keep else tail
        dp = lax.dot_general(v, do, (((1,), (1,)), ((), ())), preferred_element_type=F32)
        ds = (p * (dp - delta)).astype(BF16)
        dv = jnp.dot(p.astype(BF16), do, preferred_element_type=F32)
        dk = jnp.dot(ds, q, preferred_element_type=F32)
        dq = lax.dot_general(k, ds, (((0,), (0,)), ((), ())), preferred_element_type=F32)
        return dk, dv, dq

    def suffix(g):
        for copy in large[g]:
            copy.wait()
        key_pos = lax.broadcasted_iota(jnp.int32, (CHUNK, n), 0)
        row_pos = lax.shift_right_logical(lax.broadcasted_iota(jnp.int32, (CHUNK, n), 1), 3)
        mask = key_pos <= row_pos
        tail_acc[...] = jnp.zeros_like(tail_acc)
        for c in range(chunks):
            nk = CHUNK * (c + 1)
            lse, delta = spread(lse_s, g, CHUNK * c, heads), spread(delta_s, g, CHUNK * c, heads)
            rows_s[0, g, c] = lse
            rows_s[1, g, c] = delta
            q = q_s[g, CHUNK * c : CHUNK * c + CHUNK].reshape(n, depth)
            do = do_s[g, CHUNK * c : CHUNK * c + CHUNK].reshape(n, depth)
            dk, dv, dq = piece(bkv[0, g, :nk], bkv[1, g, :nk], q, do, lse, delta, mask)
            tail_acc[0, :nk] += dk
            tail_acc[1, :nk] += dv
            dq_acc[g, c] = dq
        bout[0, pl.ds(g, seq, stride=groups), :] = tail_acc[0] * scale
        bout[1, pl.ds(g, seq, stride=groups), :] = tail_acc[1]

    def prompt_chunks(g, first, count):
        def body(c, _):
            at = pl.ds(pl.multiple_of(c * CHUNK, CHUNK), CHUNK)
            k = kv[0, g].reshape(prompt, depth)
            v = kv[1, g].reshape(prompt, depth)
            q = q_s[g, at].reshape(n, depth)
            do = do_s[g, at].reshape(n, depth)
            dk, dv, dq = piece(k, v, q, do, rows_s[0, g, c], rows_s[1, g, c], None)
            acc[0] += dk
            acc[1] += dv
            dq = ((dq + dq_acc[g, c]) * scale).T.astype(BF16)
            dq_s[g, at] = dq.reshape(CHUNK, heads, depth)
            return 0

        lax.fori_loop(first, first + count, body, 0, unroll=UNROLL)

    def line_done():
        whole = remote(line.at[:7], line.at[:7], line_sem.at[0], line_sem.at[1], sibling, h)
        whole.wait_recv()
        whole.wait_send()
        line_f[...] = line[...].reshape(8 * 32, depth).astype(F32)
        for g in range(groups):
            kv[core, g, plane] = line_f[pl.ds(h * groups + g, 32, stride=2 * groups), :].astype(BF16)
            for d in range(1, 16):
                block = kv.at[core, g, plane]
                remote(block, block, plane_sem.at[0, g], plane_sem.at[1, g], plane_peer(d), h).start()

    def forward(g):
        blocks = kv.at[core, g, :15]
        remote(blocks, blocks, plane_sem.at[0, g], plane_sem.at[1, g], sibling, h).wait_recv()
        remote(kv.at[core, g], kv.at[core, g], fwd_sem.at[0, g], fwd_sem.at[1, g], sibling, h).start()

    def forwarded(g):
        remote(kv.at[1 - core, g], kv.at[1 - core, g], fwd_sem.at[0, g], fwd_sem.at[1, g], sibling, h).wait_recv()

    def pair_copy(g):
        return remote(half.at[g, 1 - core], half_in.at[g], pair_sem.at[0, g], pair_sem.at[1, g], sibling, h)

    def pair_start(g):
        half[g, 0] = (acc[0] * scale).astype(BF16)
        half[g, 1] = acc[1].astype(BF16)
        pair[g] = acc[core] * jnp.where(core == 0, scale, 1.0)
        pair_copy(g).start()

    def plane_start(g):
        pair_copy(g).wait_recv()
        total = pair[g] + half_in[g].astype(F32)
        spot[g] = total.astype(BF16).reshape(16, 32, depth)
        for d in range(1, 16):
            to = (plane + d) % 16
            remote(spot.at[g, to], spot_in.at[g, plane], red_sem.at[0, g], red_sem.at[1, g], plane_peer(d), h).start()
        spot_in[g, plane] = spot[g, plane]

    def plane_done(g):
        blocks = spot_in.at[g, :15]
        remote(blocks, blocks, red_sem.at[0, g], red_sem.at[1, g], sibling, h).wait_recv()
        owned[...] = jnp.sum(spot_in[g].astype(F32), axis=0)
        for o in range(8):
            fin[o, 4 * g : 4 * g + 4] = owned[4 * o : 4 * o + 4]

    for g in range(2):
        suffix(g)
    line_done()
    for g in range(2, groups):
        suffix(g)
    branch_out = [pltpu.make_async_copy(fin_b.at[i], out, out_sem.at[groups + i]) for i, out in enumerate((dbk_hbm, dbv_hbm))]
    for i in range(2):
        fin_b[i] = bout[i].astype(BF16)
        branch_out[i].start()
    forward(0)
    forwarded(0)
    dq_out = [pltpu.make_async_copy(dq_s.at[g], dq_hbm.at[:, g], out_sem.at[g]) for g in range(groups)]
    for g in range(groups):
        acc[...] = jnp.zeros_like(acc)
        prompt_chunks(g, 0, chunks // 2)
        if g + 1 < groups:
            forward(g + 1)
        if g:
            plane_start(g - 1)
        prompt_chunks(g, chunks // 2, chunks // 2)
        pair_start(g)
        dq_out[g].start()
        if g + 1 < groups:
            forwarded(g + 1)
        if g > 1:
            plane_done(g - 2)
    plane_start(groups - 1)
    plane_done(groups - 2)
    plane_done(groups - 1)
    for o in range(8):
        owner_out[o] = fin[o].astype(BF16)
    for d in range(1, 8):
        other, pb, ph = line_peer(d)
        remote(owner_out.at[other], owner_in.at[place], own_sem.at[0], own_sem.at[1], pb, ph).start()
    owner_in[place] = owner_out[place]
    whole = remote(owner_in.at[:7], owner_in.at[:7], own_sem.at[0], own_sem.at[1], sibling, h)
    whole.wait_recv()
    prompt_out = []
    for kind, out in enumerate((dpk_hbm, dpv_hbm)):
        for x in range(2):
            owned[:16] = owner_in[2 * kind + x].astype(F32) + owner_in[4 + 2 * kind + x].astype(F32)
            for s in range(4):
                line_f[32 * kind + 8 * s + 4 * x : 32 * kind + 8 * s + 4 * x + 4] = owned[pl.ds(s, 4, stride=4), :]
        own_s[kind] = line_f[32 * kind : 32 * kind + 32].astype(BF16)
        copy = pltpu.make_async_copy(own_s.at[kind], out, in_sem.at[kind])
        copy.start()
        prompt_out.append(copy)

    whole.wait_send()
    for g in range(groups):
        blocks = spot.at[g, :15]
        remote(blocks, blocks, red_sem.at[0, g], red_sem.at[1, g], sibling, h).wait_send()
        pair_copy(g).wait_send()
        blocks = kv.at[core, g, :15]
        remote(blocks, blocks, plane_sem.at[0, g], plane_sem.at[1, g], sibling, h).wait_send()
        remote(kv.at[core, g], kv.at[core, g], fwd_sem.at[0, g], fwd_sem.at[1, g], sibling, h).wait_send()
    for copy in branch_out + dq_out + prompt_out:
        copy.wait()


def shards(queries, grad_out, branch_keys, branch_values, row_lse, row_delta, lengths, prompt_keys, prompt_values):
    seq, head_count, depth = queries.shape[1:]
    groups = branch_keys.shape[2]
    heads = head_count // groups
    all_groups = prompt_keys.shape[1]
    own = prompt_keys.shape[0]
    prompt = own * lax.axis_size("branch") * lax.axis_size("head")
    scale = 1.0 / math.sqrt(depth)
    vm, sem = pltpu.VMEM, pltpu.SemaphoreType.DMA
    any_space = pl.BlockSpec(memory_space=pl.ANY)

    def body(*refs):
        kernel(seq, groups, heads, prompt, depth, scale, *refs)

    dq, dbk, dbv, dpk, dpv = pl.pallas_call(
        body,
        out_shape=[
            jax.ShapeDtypeStruct((seq, groups, heads, depth), BF16),
            jax.ShapeDtypeStruct((seq * groups, depth), BF16),
            jax.ShapeDtypeStruct((seq * groups, depth), BF16),
            jax.ShapeDtypeStruct((own * all_groups, depth), BF16),
            jax.ShapeDtypeStruct((own * all_groups, depth), BF16),
        ],
        in_specs=[pl.BlockSpec(memory_space=pltpu.SMEM)] + [any_space] * 8,
        out_specs=[any_space] * 5,
        scratch_shapes=[
            vm((groups, seq, heads, depth), BF16),
            vm((groups, seq, heads, depth), BF16),
            vm((groups, seq, heads, depth), BF16),
            vm((groups, seq // CHUNK, depth, CHUNK * heads), F32),
            vm((head_count, seq), F32),
            vm((head_count, seq), F32),
            vm((2, groups, seq // CHUNK, 1, CHUNK * heads), F32),
            vm((2, own * all_groups, depth), BF16),
            vm((2, seq * groups, depth), BF16),
            vm((2, groups, seq, depth), BF16),
            vm((seq * groups, depth), F32),
            vm((2, groups, 16, prompt // 16, depth), BF16),
            vm((8, own * all_groups, depth), BF16),
            vm((8 * own * all_groups, depth), F32),
            vm((2, prompt, depth), F32),
            vm((2, seq, depth), F32),
            vm((groups, prompt, depth), F32),
            vm((groups, 2, prompt, depth), BF16),
            vm((groups, prompt, depth), BF16),
            vm((groups, 16, prompt // 16, depth), BF16),
            vm((groups, 16, prompt // 16, depth), BF16),
            vm((prompt // 16, depth), F32),
            vm((8, groups * own, depth), BF16),
            vm((8, groups * own, depth), BF16),
            vm((8, groups * own, depth), F32),
            vm((2, seq * groups, depth), BF16),
            vm((2, seq * groups, depth), F32),
            sem((6,)), sem((2, groups)), sem((groups + 2,)), sem((2,)), sem((2, groups)),
            sem((2, groups)), sem((2, groups)), sem((2, groups)), sem((2,)),
        ],
        compiler_params=pltpu.CompilerParams(
            collective_id=0, has_side_effects=True, vmem_limit_bytes=60 * 1024 * 1024
        ),
    )(
        lengths,
        queries.reshape(seq, groups, heads, depth),
        grad_out.reshape(seq, groups, heads, depth),
        row_lse[0],
        row_delta[0],
        prompt_keys.reshape(own * all_groups, depth),
        prompt_values.reshape(own * all_groups, depth),
        branch_keys.reshape(seq * groups, depth),
        branch_values.reshape(seq * groups, depth),
    )
    return (
        dq.reshape(queries.shape),
        dbk.reshape(branch_keys.shape),
        dbv.reshape(branch_values.shape),
        dpk.reshape(prompt_keys.shape),
        dpv.reshape(prompt_values.shape),
    )


def solution(mesh):
    whole = P("branch", None, "head", None)
    rows = P("branch", "head", None)
    prompt = P(("branch", "head"), None, None)
    return jax.shard_map(
        shards,
        mesh=mesh,
        in_specs=(whole, whole, whole, whole, rows, rows, P("branch"), prompt, prompt),
        out_specs=(whole, whole, whole, prompt, prompt),
        check_vma=False,
    )
```

time: 157 us -> 52.3 us (0.33)
  waiting for transfers between devices: 66 us -> 0 us
  matrix products: 46.3 us -> 0 us
  Pallas kernels: 0 us -> 44.9 us
  starting transfers between devices: 15.2 us -> 0 us
  between operations: 15 us -> 1.32 us
  local copies, waits for them, and re-layouts: 12.1 us -> 5.94 us
  other arithmetic: 1.61 us -> 0 us
    all_gather x1 -> x0, waiting for transfers between devices: 56.1 us -> none  [side_by_side(): result = lax.all_gather(both, axis, axis=dim, tiled=True)]
    dot_general x15 -> x0, matrix products: 46.3 us -> none  [the longest x3 13 us: score_pieces(): jnp.einsum('grsk,kgd->sgrd', score_grad, key_rows, preferred_element_type...]
    pallas_call x0 -> x1, Pallas kernels: none -> 44.9 us  [shards(): pl.pallas_call(body, out_shape=[jax.ShapeDtypeStruct((seq, groups, heads,...]
    all_to_all x3 -> x0, starting transfers between devices: 15.2 us -> none  [the longest x1 8.71 us: sum_at_owner(): lax.all_to_all(tiles, axis, split_axis=0, concat_axis=0, tiled=True)]
    all_to_all x3 -> x0, waiting for transfers between devices: 9.89 us -> none  [the longest x1 7.38 us: sum_at_owner(): lax.all_to_all(tiles, axis, split_axis=0, concat_axis=0, tiled=True)]
    unnamed x31 -> x13, local copies, waits for them, and re-layouts: 10.2 us -> 5.94 us
    concatenate x2 -> x0, local copies, waits for them, and re-layouts: 1.88 us -> none  [the longest x1 1.27 us: in_one_piece(): both = jnp.concatenate(arrays, axis=along)]
  transfers between devices with their start and end apart: 4 -> 0, of which waited for: 3 -> 0; matrix products, arithmetic and copies ran while one was open for 22% -> 0% of each run, Pallas kernels for 0% -> 0%
where the time goes in v1:
time: 52.3 us; the launch traced here: 52.1 us
  Pallas kernels  44.9 us (86%)
  local copies, waits for them, and re-layouts  5.94 us (11%)
  between operations  1.32 us (3%)
    pallas_call x1, Pallas kernels, shards(): pl.pallas_call(body, out_shape=[jax.ShapeDtypeStruct((seq, groups, heads,...  44.9 us
    unnamed x13, local copies, waits for them, and re-layouts  5.94 us

profile of v1, /device:TPU:1, one launch (start us, length us, event | category | flops | bytes accessed | tf_op | source)
XLA Modules:
  0.0 52.1 jit_solution(13787265457853821016)
XLA Ops:
  1.3 44.9 %shard_map.128 = (bf16[256,4,8,128]{3,2,1,0:T(8,128)(2,1)}, bf16[1024,128]{1,0:T(8,128)(2,1)}, bf16[1024,128]{1,0:T(8,128)(2,1)}, bf16[32,128]{1,0:T(8,128)(2,1)}, bf16[32,128]{1,0:T(8,128)(2,1)}) custom-call(s32[1]{0:T(128)S(6)} %copy.19.refs_0_, bf16[256,4,8,128]{3,2,1,0:T(8,128)(2,1)} %bitcast.13, bf16[256,4,8,128]{3,2,1,0:T(8,128)(2,1)} %bitcast.14, ...), custom_call_target="tpu_custom_call" | custom-call | tf_op jit(solution)/shard_map/pallas_call | solution.py:280
  46.2 0.0 copy-start.1
  46.2 0.0 copy-start
  46.2 0.0 copy-start.3
  46.2 0.0 copy-start.2
  46.2 3.3 %copy.20 = bf16[1,256,32,128]{3,2,1,0:T(8,128)(2,1)} copy(bf16[1,256,32,128]{3,2,1,0:T(8,128)(2,1)} %bitcast.15) | data formatting | bytes 4194304
  49.5 0.0 copy-done.1
  49.5 0.7 %copy.21 = bf16[1,256,4,128]{3,2,1,0:T(4,128)(2,1)} copy(bf16[1,256,4,128]{3,2,1,0:T(4,128)(2,1)S(1)} %bitcast.19) | data formatting | bytes 524288
  50.2 0.0 copy-done
  50.2 0.7 %copy.22 = bf16[1,256,4,128]{3,2,1,0:T(4,128)(2,1)} copy(bf16[1,256,4,128]{3,2,1,0:T(4,128)(2,1)S(1)} %bitcast.18) | data formatting | bytes 524288
  50.9 0.0 copy-done.3
  50.9 0.6 %copy.23 = bf16[4,8,128]{2,1,0:T(8,128)(2,1)} copy(bf16[4,8,128]{2,1,0:T(8,128)(2,1)S(1)} %bitcast.25) | data formatting | bytes 16384
  51.5 0.0 copy-done.2
  51.5 0.6 %copy.24 = bf16[4,8,128]{2,1,0:T(8,128)(2,1)} copy(bf16[4,8,128]{2,1,0:T(8,128)(2,1)S(1)} %bitcast.24) | data formatting | bytes 16384
Async XLA Ops:
  46.2 3.4 %copy-start.1 = (bf16[1024,128]{1,0:T(8,128)(2,1)S(1)}, bf16[1024,128]{1,0:T(8,128)(2,1)}, u32[]{:S(2)}) copy-start(bf16[1024,128]{1,0:T(8,128)(2,1)} %get-tuple-element.11) | copy-start | bytes 786436
  46.2 4.1 %copy-start = (bf16[1024,128]{1,0:T(8,128)(2,1)S(1)}, bf16[1024,128]{1,0:T(8,128)(2,1)}, u32[]{:S(2)}) copy-start(bf16[1024,128]{1,0:T(8,128)(2,1)} %get-tuple-element.12) | copy-start | bytes 786436
  46.2 4.8 %copy-start.3 = (bf16[32,128]{1,0:T(8,128)(2,1)S(1)}, bf16[32,128]{1,0:T(8,128)(2,1)}, u32[]{:S(2)}) copy-start(bf16[32,128]{1,0:T(8,128)(2,1)} %get-tuple-element.13) | copy-start | bytes 24580
  46.2 5.3 %copy-start.2 = (bf16[32,128]{1,0:T(8,128)(2,1)S(1)}, bf16[32,128]{1,0:T(8,128)(2,1)}, u32[]{:S(2)}) copy-start(bf16[32,128]{1,0:T(8,128)(2,1)} %get-tuple-element.14) | copy-start | bytes 24580

commit v2 on v1

v2 whole, which is shorter than its diff:
```python
import math

import jax
import jax.numpy as jnp
from jax import lax
from jax.experimental import pallas as pl
from jax.experimental.pallas import tpu as pltpu
from jax.sharding import PartitionSpec as P

F32 = jnp.float32
BF16 = jnp.bfloat16
LOG2E = math.log2(math.e)
CHUNK = 32
PLANE = sorted(((i, j) for i in range(4) for j in range(4) if i or j), key=lambda s: -sum(min(k, 4 - k) for k in s))


def remote(src, dst, send_sem, recv_sem, branch, head):
    return pltpu.make_async_remote_copy(
        src_ref=src,
        dst_ref=dst,
        send_sem=send_sem,
        recv_sem=recv_sem,
        device_id={"branch": branch, "head": head},
        device_id_type=pl.DeviceIdType.MESH,
    )


def spread(ref, group, pos, heads):
    row = lax.broadcasted_iota(jnp.int32, (heads, 128), 0)
    lane = lax.broadcasted_iota(jnp.int32, (heads, 128), 1)
    step = 128 // heads
    tile = ref[heads * group : heads * group + heads, pos // 128 * 128 : pos // 128 * 128 + 128]
    outs = []
    for k in range(CHUNK // step):
        index = lax.shift_right_logical(lane, 3) + (pos % 128 + step * k)
        picked = jnp.take_along_axis(tile, index, axis=1, mode="promise_in_bounds")
        picked = jnp.where(row == (lane & (heads - 1)), picked, 0.0)
        outs.append(jnp.sum(picked, axis=0, keepdims=True))
    return jnp.concatenate(outs, axis=1)


def kernel(
    seq, groups, heads, prompt, depth, scale,
    length_hbm, q_hbm, do_hbm, lse_hbm, delta_hbm, pk_hbm, pv_hbm, bk_hbm, bv_hbm,
    dq_s, fin_b, owner_in,
    q_s, do_s, dq_acc, ds_s, lse_s, delta_s, rows_s, own_s, bin_s, bkv, wide, kv,
    line, line_f, acc, tail_acc, pair, half, half_in, spot, spot_in, owned, owner_out, fin,
    bout, length_s, in_sem, q_sem, line_sem, plane_sem, fwd_sem, pair_sem, red_sem, own_sem,
):
    b, h = lax.axis_index("branch"), lax.axis_index("head")
    plane, place = b // 4, (b % 4) * 2 + h
    core = b % 2
    sibling = b + 1 - 2 * core
    chunks = seq // CHUNK
    n = CHUNK * heads
    exp_scale = scale * LOG2E

    def plane_peer(step):
        other = (plane // 4 + step[0]) % 4 * 4 + (plane % 4 + step[1]) % 4
        return other, other * 4 + b % 4

    def line_peer(d):
        other = (place + d) % 8
        return other, plane * 4 + other // 2, other % 2

    barrier = pltpu.get_barrier_semaphore()
    for d in range(1, 8):
        _, pb, ph = line_peer(d)
        pl.semaphore_signal(barrier, inc=1, device_id={"branch": pb, "head": ph}, device_id_type=pl.DeviceIdType.MESH)
    for step in PLANE:
        pl.semaphore_signal(barrier, inc=1, device_id={"branch": plane_peer(step)[1], "head": h}, device_id_type=pl.DeviceIdType.MESH)

    small = [
        pltpu.make_async_copy(src, dst, in_sem.at[i])
        for i, (src, dst) in enumerate(
            (
                (pk_hbm, own_s.at[0]), (pv_hbm, own_s.at[1]), (lse_hbm, lse_s), (delta_hbm, delta_s),
                (bk_hbm, bin_s.at[0]), (bv_hbm, bin_s.at[1]), (length_hbm, length_s),
            )
        )
    ]
    large = [
        (
            pltpu.make_async_copy(q_hbm.at[:, g], q_s.at[g], q_sem.at[0, g]),
            pltpu.make_async_copy(do_hbm.at[:, g], do_s.at[g], q_sem.at[1, g]),
        )
        for g in range(groups)
    ]
    for copy in small:
        copy.start()
    for pair_of in large:
        for copy in pair_of:
            copy.start()
    small[0].wait()
    small[1].wait()
    pl.semaphore_wait(barrier, 22)

    for d in range(1, 8):
        other, pb, ph = line_peer(d)
        remote(own_s.at[other // 2 % 2], line.at[place], line_sem.at[0], line_sem.at[1], pb, ph).start()
    line[place] = own_s[core]

    for copy in small[2:]:
        copy.wait()
    position = lax.broadcasted_iota(jnp.int32, (groups * heads, seq), 1)
    lse_s[...] = jnp.where(position < length_s[0], lse_s[...] * LOG2E, 1e30)
    for kind in range(2):
        wide[...] = bin_s[kind].astype(F32)
        for g in range(groups):
            bkv[kind, g] = wide[pl.ds(g, seq, stride=groups), :].astype(BF16)

    def piece(k, v, q, do, lse, delta, mask):
        st = lax.dot_general(k, q, (((1,), (1,)), ((), ())), preferred_element_type=F32)
        p = jnp.exp2(st * exp_scale - lse)
        if mask is not None:
            keep = k.shape[0] - CHUNK
            tail = jnp.where(mask, p[keep:], 0.0)
            p = jnp.concatenate([p[:keep], tail], axis=0) if keep else tail
        dp = lax.dot_general(v, do, (((1,), (1,)), ((), ())), preferred_element_type=F32)
        ds = (p * (dp - delta)).astype(BF16)
        dv = jnp.dot(p.astype(BF16), do, preferred_element_type=F32)
        dk = jnp.dot(ds, q, preferred_element_type=F32)
        return dk, dv, ds

    def suffix(g, first, last):
        if first == 0:
            for copy in large[g]:
                copy.wait()
            tail_acc[...] = jnp.zeros_like(tail_acc)
        key_pos = lax.broadcasted_iota(jnp.int32, (CHUNK, n), 0)
        row_pos = lax.shift_right_logical(lax.broadcasted_iota(jnp.int32, (CHUNK, n), 1), 3)
        mask = key_pos <= row_pos
        for c in range(first, last):
            nk = CHUNK * (c + 1)
            lse, delta = spread(lse_s, g, CHUNK * c, heads), spread(delta_s, g, CHUNK * c, heads)
            rows_s[0, g, c] = lse
            rows_s[1, g, c] = delta
            q = q_s[g, CHUNK * c : CHUNK * c + CHUNK].reshape(n, depth)
            do = do_s[g, CHUNK * c : CHUNK * c + CHUNK].reshape(n, depth)
            k = bkv[0, g, :nk]
            dk, dv, ds = piece(k, bkv[1, g, :nk], q, do, lse, delta, mask)
            tail_acc[0, :nk] += dk
            tail_acc[1, :nk] += dv
            dq_acc[g, c] = lax.dot_general(k, ds, (((0,), (0,)), ((), ())), preferred_element_type=F32)
        if last < chunks:
            return
        bout[0, pl.ds(g, seq, stride=groups), :] = tail_acc[0] * scale
        bout[1, pl.ds(g, seq, stride=groups), :] = tail_acc[1]

    def prompt_chunks(g, first, last):
        k = kv[0, g].reshape(prompt, depth)
        v = kv[1, g].reshape(prompt, depth)
        for c in range(first, last):
            q = q_s[g, CHUNK * c : CHUNK * c + CHUNK].reshape(n, depth)
            do = do_s[g, CHUNK * c : CHUNK * c + CHUNK].reshape(n, depth)
            dk, dv, ds = piece(k, v, q, do, rows_s[0, g, c], rows_s[1, g, c], None)
            ds_s[g, c] = ds
            if c:
                acc[0] += dk
                acc[1] += dv
            else:
                acc[0] = dk
                acc[1] = dv

    def query_part(g):
        k = kv[0, g].reshape(prompt, depth)
        for c in range(chunks):
            dq = lax.dot_general(k, ds_s[g, c], (((0,), (0,)), ((), ())), preferred_element_type=F32)
            dq = ((dq + dq_acc[g, c]) * scale).T.astype(BF16)
            dq_s[g, CHUNK * c : CHUNK * c + CHUNK] = dq.reshape(CHUNK, heads, depth)

    def line_done():
        whole = remote(line.at[:7], line.at[:7], line_sem.at[0], line_sem.at[1], sibling, h)
        whole.wait_recv()
        whole.wait_send()
        line_f[...] = line[...].reshape(8 * 32, depth).astype(F32)
        for g in range(groups):
            kv[core, g, plane] = line_f[pl.ds(h * groups + g, 32, stride=2 * groups), :].astype(BF16)

    def plane_send(g):
        block = kv.at[core, g, plane]
        for step in PLANE:
            remote(block, block, plane_sem.at[0, g], plane_sem.at[1, g], plane_peer(step)[1], h).start()

    def forward(g):
        blocks = kv.at[core, g, :15]
        remote(blocks, blocks, plane_sem.at[0, g], plane_sem.at[1, g], sibling, h).wait_recv()
        remote(kv.at[core, g], kv.at[core, g], fwd_sem.at[0, g], fwd_sem.at[1, g], sibling, h).start()

    def forwarded(g):
        remote(kv.at[1 - core, g], kv.at[1 - core, g], fwd_sem.at[0, g], fwd_sem.at[1, g], sibling, h).wait_recv()

    def pair_copy(g):
        return remote(half.at[g, 1 - core], half_in.at[g], pair_sem.at[0, g], pair_sem.at[1, g], sibling, h)

    def pair_start(g):
        half[g, 0] = (acc[0] * scale).astype(BF16)
        half[g, 1] = acc[1].astype(BF16)
        pair[g] = acc[core] * jnp.where(core == 0, scale, 1.0)
        pair_copy(g).start()

    def plane_start(g):
        pair_copy(g).wait_recv()
        total = pair[g] + half_in[g].astype(F32)
        spot[g] = total.astype(BF16).reshape(16, 32, depth)
        for step in PLANE:
            to, pb = plane_peer(step)
            remote(spot.at[g, to], spot_in.at[g, plane], red_sem.at[0, g], red_sem.at[1, g], pb, h).start()
        spot_in[g, plane] = spot[g, plane]

    def plane_done(g):
        blocks = spot_in.at[g, :15]
        remote(blocks, blocks, red_sem.at[0, g], red_sem.at[1, g], sibling, h).wait_recv()
        owned[...] = jnp.sum(spot_in[g].astype(F32), axis=0)
        for o in range(8):
            fin[o, 4 * g : 4 * g + 4] = owned[4 * o : 4 * o + 4]

    suffix(0, 0, chunks)
    suffix(1, 0, chunks // 2)
    line_done()
    plane_send(0)
    plane_send(1)
    suffix(1, chunks // 2, chunks)
    suffix(2, 0, chunks)
    suffix(3, 0, chunks // 2)
    forward(0)
    plane_send(2)
    plane_send(3)
    suffix(3, chunks // 2, chunks)
    for i in range(2):
        fin_b[i] = bout[i].astype(BF16)
    forwarded(0)
    prompt_chunks(0, 0, chunks // 2)
    forward(1)
    prompt_chunks(0, chunks // 2, chunks)
    pair_start(0)
    for g in range(1, groups):
        forwarded(g)
        if g == 1:
            prompt_chunks(g, 0, chunks // 2)
            forward(g + 1)
            prompt_chunks(g, chunks // 2, chunks)
        else:
            if g + 1 < groups:
                forward(g + 1)
            prompt_chunks(g, 0, chunks)
        pair_start(g)
        plane_start(g - 1)
    query_part(0)
    plane_start(groups - 1)
    for g in range(1, groups):
        query_part(g)
    for g in range(groups):
        plane_done(g)
    for o in range(8):
        owner_out[o] = fin[o].astype(BF16)
    for d in range(1, 8):
        other, pb, ph = line_peer(d)
        remote(owner_out.at[other], owner_in.at[place], own_sem.at[0], own_sem.at[1], pb, ph).start()
    owner_in[place] = owner_out[place]
    whole = remote(owner_in.at[:7], owner_in.at[:7], own_sem.at[0], own_sem.at[1], sibling, h)
    whole.wait_recv()
    whole.wait_send()
    for g in range(groups):
        blocks = spot.at[g, :15]
        remote(blocks, blocks, red_sem.at[0, g], red_sem.at[1, g], sibling, h).wait_send()
        pair_copy(g).wait_send()
        blocks = kv.at[core, g, :15]
        remote(blocks, blocks, plane_sem.at[0, g], plane_sem.at[1, g], sibling, h).wait_send()
        remote(kv.at[core, g], kv.at[core, g], fwd_sem.at[0, g], fwd_sem.at[1, g], sibling, h).wait_send()


def write_out(dq_s, branch_s, owner_in, dq_hbm, dbk_hbm, dbv_hbm, dpk_hbm, dpv_hbm, owned, rows, rows_b, sems):
    groups = dq_s.shape[0]
    copies = [pltpu.make_async_copy(dq_s.at[g], dq_hbm.at[:, g], sems.at[g]) for g in range(groups)]
    for kind, out in enumerate((dbk_hbm, dbv_hbm)):
        copies.append(pltpu.make_async_copy(branch_s.at[kind], out, sems.at[groups + kind]))
    for copy in copies:
        copy.start()
    for kind in range(2):
        for x in range(2):
            owned[...] = owner_in[2 * kind + x].astype(F32) + owner_in[4 + 2 * kind + x].astype(F32)
            for s in range(4):
                rows[kind, 8 * s + 4 * x : 8 * s + 4 * x + 4] = owned[pl.ds(s, 4, stride=4), :]
    rows_b[...] = rows[...].astype(BF16)
    for kind, out in enumerate((dpk_hbm, dpv_hbm)):
        copies.append(pltpu.make_async_copy(rows_b.at[kind], out, sems.at[groups + 2 + kind]))
        copies[-1].start()
    for copy in copies:
        copy.wait()


def shards(queries, grad_out, branch_keys, branch_values, row_lse, row_delta, lengths, prompt_keys, prompt_values):
    seq, head_count, depth = queries.shape[1:]
    groups = branch_keys.shape[2]
    heads = head_count // groups
    all_groups = prompt_keys.shape[1]
    own = prompt_keys.shape[0]
    prompt = own * lax.axis_size("branch") * lax.axis_size("head")
    scale = 1.0 / math.sqrt(depth)
    vm, sem = pltpu.VMEM, pltpu.SemaphoreType.DMA
    any_space = pl.BlockSpec(memory_space=pl.ANY)
    in_vmem = pl.BlockSpec(memory_space=pltpu.VMEM)

    def body(*refs):
        kernel(seq, groups, heads, prompt, depth, scale, *refs)

    results = pl.pallas_call(
        body,
        out_shape=[
            vm((groups, seq, heads, depth), BF16),
            vm((2, seq * groups, depth), BF16),
            vm((8, groups * own, depth), BF16),
        ],
        in_specs=[any_space] * 9,
        out_specs=[in_vmem] * 3,
        scratch_shapes=[
            vm((groups, seq, heads, depth), BF16),
            vm((groups, seq, heads, depth), BF16),
            vm((groups, seq // CHUNK, depth, CHUNK * heads), F32),
            vm((groups, seq // CHUNK, prompt, CHUNK * heads), BF16),
            vm((head_count, seq), F32),
            vm((head_count, seq), F32),
            vm((2, groups, seq // CHUNK, 1, CHUNK * heads), F32),
            vm((2, own * all_groups, depth), BF16),
            vm((2, seq * groups, depth), BF16),
            vm((2, groups, seq, depth), BF16),
            vm((seq * groups, depth), F32),
            vm((2, groups, 16, prompt // 16, depth), BF16),
            vm((8, own * all_groups, depth), BF16),
            vm((8 * own * all_groups, depth), F32),
            vm((2, prompt, depth), F32),
            vm((2, seq, depth), F32),
            vm((groups, prompt, depth), F32),
            vm((groups, 2, prompt, depth), BF16),
            vm((groups, prompt, depth), BF16),
            vm((groups, 16, prompt // 16, depth), BF16),
            vm((groups, 16, prompt // 16, depth), BF16),
            vm((prompt // 16, depth), F32),
            vm((8, groups * own, depth), BF16),
            vm((8, groups * own, depth), F32),
            vm((2, seq * groups, depth), F32),
            pltpu.SMEM((1,), jnp.int32),
            sem((7,)), sem((2, groups)), sem((2,)), sem((2, groups)),
            sem((2, groups)), sem((2, groups)), sem((2, groups)), sem((2,)),
        ],
        compiler_params=pltpu.CompilerParams(
            collective_id=0, has_side_effects=True, vmem_limit_bytes=48 * 1024 * 1024
        ),
    )(
        lengths,
        *(
            pltpu.with_memory_space_constraint(a, pltpu.HBM)
            for a in (
                queries.reshape(seq, groups, heads, depth),
                grad_out.reshape(seq, groups, heads, depth),
                row_lse[0],
                row_delta[0],
                prompt_keys.reshape(own * all_groups, depth),
                prompt_values.reshape(own * all_groups, depth),
                branch_keys.reshape(seq * groups, depth),
                branch_values.reshape(seq * groups, depth),
            )
        ),
    )
    dq, dbk, dbv, dpk, dpv = pl.pallas_call(
        write_out,
        out_shape=[
            jax.ShapeDtypeStruct((seq, groups, heads, depth), BF16),
            jax.ShapeDtypeStruct((seq * groups, depth), BF16),
            jax.ShapeDtypeStruct((seq * groups, depth), BF16),
            jax.ShapeDtypeStruct((own * all_groups, depth), BF16),
            jax.ShapeDtypeStruct((own * all_groups, depth), BF16),
        ],
        in_specs=[in_vmem] * 3,
        out_specs=[any_space] * 5,
        scratch_shapes=[
            vm((groups * own, depth), F32),
            vm((2, own * all_groups, depth), F32),
            vm((2, own * all_groups, depth), BF16),
            sem((groups + 4,)),
        ],
        compiler_params=pltpu.CompilerParams(vmem_limit_bytes=8 * 1024 * 1024),
    )(*results)
    return (
        dq.reshape(queries.shape),
        dbk.reshape(branch_keys.shape),
        dbv.reshape(branch_values.shape),
        dpk.reshape(prompt_keys.shape),
        dpv.reshape(prompt_values.shape),
    )


def solution(mesh):
    whole = P("branch", None, "head", None)
    rows = P("branch", "head", None)
    prompt = P(("branch", "head"), None, None)
    return jax.shard_map(
        shards,
        mesh=mesh,
        in_specs=(whole, whole, whole, whole, rows, rows, P("branch"), prompt, prompt),
        out_specs=(whole, whole, whole, prompt, prompt),
        check_vma=False,
    )
```

time: 52.3 us -> 42.4 us (0.81)
  local copies, waits for them, and re-layouts: 5.94 us -> 0 us
  Pallas kernels: 44.9 us -> 40.9 us
    unnamed x13 -> x0, local copies, waits for them, and re-layouts: 5.94 us -> none
    pallas_call x1 -> x2, Pallas kernels: 44.9 us -> 40.9 us  [the longest x1 39.3 us: shards(): pl.pallas_call(body, out_shape=[vm((groups, seq, heads, depth), BF16), vm...]
where the time goes in v2:
time: 42.4 us; the launch traced here: 42.3 us
  Pallas kernels  40.9 us (96%)
  between operations  1.45 us (3%)
    pallas_call x1, Pallas kernels, shards(): pl.pallas_call(body, out_shape=[vm((groups, seq, heads, depth), BF16), vm...  39.3 us
    pallas_call x1, Pallas kernels, shards(): pl.pallas_call(write_out, out_shape=[jax.ShapeDtypeStruct((seq, groups, h...  1.56 us

profile of v2, /device:TPU:1, one launch (start us, length us, event | category | flops | bytes accessed | tf_op | source)
XLA Modules:
  0.0 42.3 jit_solution(793409819418161435)
XLA Ops:
  1.3 39.3 %shard_map.128 = (bf16[4,256,8,128]{3,2,1,0:T(8,128)(2,1)S(1)}, bf16[2,1024,128]{2,1,0:T(8,128)(2,1)S(1)}, bf16[8,16,128]{2,1,0:T(8,128)(2,1)S(1)}) custom-call(s32[1]{0:T(128)S(6)} %copy.14.refs_0_, bf16[256,4,8,128]{3,2,1,0:T(8,128)(2,1)} %bitcast.13, bf16[256,4,8,128]{3,2,1,0:T(8,128)(2,1)} %bitcast.14, f32[32,256]{1,0:T(8,128)} %bitcast.17, ...), custom_call_target="tpu_custom_call" | custom-call | tf_op jit(solution)/shard_map/pallas_call | solution.py:308
  40.6 1.6 %shard_map.129 = (bf16[256,4,8,128]{3,2,1,0:T(8,128)(2,1)}, bf16[1024,128]{1,0:T(8,128)(2,1)}, bf16[1024,128]{1,0:T(8,128)(2,1)}, bf16[32,128]{1,0:T(8,128)(2,1)}, bf16[32,128]{1,0:T(8,128)(2,1)}) custom-call(bf16[4,256,8,128]{3,2,1,0:T(8,128)(2,1)S(1)} %get-tuple-element.13.dq_s, bf16[2,1024,128]{2,1,0:T(8,128)(2,1)S(1)} %get-tuple-element.14.branch_s, ...), custom_call_target="tpu_custom_call" | custom-call | tf_op jit(solution)/shard_map/pallas_call | solution.py:366

commit v3 on v2

--- a/solution.py
+++ b/solution.py
@@ -11,7 +11,15 @@
 BF16 = jnp.bfloat16
 LOG2E = math.log2(math.e)
 CHUNK = 32
-PLANE = sorted(((i, j) for i in range(4) for j in range(4) if i or j), key=lambda s: -sum(min(k, 4 - k) for k in s))
+WIDE = 2
+QWIDE = 2
+SLOTS = (
+    (0, 0), (0, 1), (0, 3), (1, 0), (3, 0), (2, 0), (1, 1), (3, 3),
+    (0, 2), (1, 3), (3, 1), (1, 2), (3, 2), (2, 1), (2, 3), (2, 2),
+)
+NEAR, ALL = 8, 16
+SPLIT = 2
+UNITS = ((0, 0, ALL), (1, 0, ALL), (2, 0, ALL), (3, NEAR, ALL), (3, 0, NEAR))
 
 
 def remote(src, dst, send_sem, recv_sem, branch, head):
@@ -43,9 +51,9 @@
     seq, groups, heads, prompt, depth, scale,
     length_hbm, q_hbm, do_hbm, lse_hbm, delta_hbm, pk_hbm, pv_hbm, bk_hbm, bv_hbm,
     dq_s, fin_b, owner_in,
-    q_s, do_s, dq_acc, ds_s, lse_s, delta_s, rows_s, own_s, bin_s, bkv, wide, kv,
+    q_s, do_s, turned, dq_acc, ds_s, lse_s, delta_s, rows_s, own_s, bin_s, bkv, wide, kv,
     line, line_f, acc, tail_acc, pair, half, half_in, spot, spot_in, owned, owner_out, fin,
-    bout, length_s, in_sem, q_sem, line_sem, plane_sem, fwd_sem, pair_sem, red_sem, own_sem,
+    bout, length_s, in_sem, q_sem, line_sem, near_sem, plane_sem, fwd_sem, pair_sem, red_sem, own_sem,
 ):
     b, h = lax.axis_index("branch"), lax.axis_index("head")
     plane, place = b // 4, (b % 4) * 2 + h
@@ -55,9 +63,14 @@
     n = CHUNK * heads
     exp_scale = scale * LOG2E
 
-    def plane_peer(step):
-        other = (plane // 4 + step[0]) % 4 * 4 + (plane % 4 + step[1]) % 4
-        return other, other * 4 + b % 4
+    def plane_peer(slot, on=None):
+        i, j = SLOTS[slot]
+        other = (plane // 4 + i) % 4 * 4 + (plane % 4 + j) % 4
+        return other * 4 + b % 4 if on is None else other * 4 + b % 4 // 2 * 2 + on
+
+    def back(slot):
+        i, j = SLOTS[slot]
+        return SLOTS.index((-i % 4, -j % 4))
 
     def line_peer(d):
         other = (place + d) % 8
@@ -67,8 +80,8 @@
     for d in range(1, 8):
         _, pb, ph = line_peer(d)
         pl.semaphore_signal(barrier, inc=1, device_id={"branch": pb, "head": ph}, device_id_type=pl.DeviceIdType.MESH)
-    for step in PLANE:
-        pl.semaphore_signal(barrier, inc=1, device_id={"branch": plane_peer(step)[1], "head": h}, device_id_type=pl.DeviceIdType.MESH)
+    for pb in [plane_peer(slot) for slot in range(1, ALL)] + [plane_peer(slot, 1 - core) for slot in range(1, NEAR)]:
+        pl.semaphore_signal(barrier, inc=1, device_id={"branch": pb, "head": h}, device_id_type=pl.DeviceIdType.MESH)
 
     small = [
         pltpu.make_async_copy(src, dst, in_sem.at[i])
@@ -93,7 +106,7 @@
             copy.start()
     small[0].wait()
     small[1].wait()
-    pl.semaphore_wait(barrier, 22)
+    pl.semaphore_wait(barrier, 29)
 
     for d in range(1, 8):
         other, pb, ph = line_peer(d)
@@ -109,65 +122,74 @@
         for g in range(groups):
             bkv[kind, g] = wide[pl.ds(g, seq, stride=groups), :].astype(BF16)
 
-    def piece(k, v, q, do, lse, delta, mask):
-        st = lax.dot_general(k, q, (((1,), (1,)), ((), ())), preferred_element_type=F32)
-        p = jnp.exp2(st * exp_scale - lse)
+    def places(c, wide):
+        return slice(CHUNK * c, CHUNK * (c + wide)), slice(n * c, n * (c + wide))
+
+    def piece(k, v, g, c, wide, mask):
+        at, lanes = places(c, wide)
+        q = q_s[g, at].reshape(n * wide, depth)
+        do = do_s[g, at].reshape(n * wide, depth)
+        st = jnp.dot(k, turned[0, g, :, lanes], preferred_element_type=F32)
+        p = jnp.exp2(st * exp_scale - rows_s[0, g, :, lanes])
         if mask is not None:
-            keep = k.shape[0] - CHUNK
+            keep = k.shape[0] - CHUNK * wide
             tail = jnp.where(mask, p[keep:], 0.0)
             p = jnp.concatenate([p[:keep], tail], axis=0) if keep else tail
-        dp = lax.dot_general(v, do, (((1,), (1,)), ((), ())), preferred_element_type=F32)
-        ds = (p * (dp - delta)).astype(BF16)
+        dp = jnp.dot(v, turned[1, g, :, lanes], preferred_element_type=F32)
+        ds = (p * (dp - rows_s[1, g, :, lanes])).astype(BF16)
         dv = jnp.dot(p.astype(BF16), do, preferred_element_type=F32)
         dk = jnp.dot(ds, q, preferred_element_type=F32)
         return dk, dv, ds
 
-    def suffix(g, first, last):
-        if first == 0:
-            for copy in large[g]:
-                copy.wait()
-            tail_acc[...] = jnp.zeros_like(tail_acc)
-        key_pos = lax.broadcasted_iota(jnp.int32, (CHUNK, n), 0)
-        row_pos = lax.shift_right_logical(lax.broadcasted_iota(jnp.int32, (CHUNK, n), 1), 3)
+    def turn(g):
+        for c in range(chunks):
+            at, lanes = places(c, 1)
+            turned[0, g, :, lanes] = q_s[g, at].reshape(n, depth).T
+            turned[1, g, :, lanes] = do_s[g, at].reshape(n, depth).T
+            rows_s[0, g, :, lanes] = spread(lse_s, g, CHUNK * c, heads)
+            rows_s[1, g, :, lanes] = spread(delta_s, g, CHUNK * c, heads)
+
+    def suffix(g):
+        for copy in large[g]:
+            copy.wait()
+        turn(g)
+        key_pos = lax.broadcasted_iota(jnp.int32, (CHUNK * WIDE, n * WIDE), 0)
+        row_pos = lax.shift_right_logical(lax.broadcasted_iota(jnp.int32, (CHUNK * WIDE, n * WIDE), 1), 3)
         mask = key_pos <= row_pos
-        for c in range(first, last):
-            nk = CHUNK * (c + 1)
-            lse, delta = spread(lse_s, g, CHUNK * c, heads), spread(delta_s, g, CHUNK * c, heads)
-            rows_s[0, g, c] = lse
-            rows_s[1, g, c] = delta
-            q = q_s[g, CHUNK * c : CHUNK * c + CHUNK].reshape(n, depth)
-            do = do_s[g, CHUNK * c : CHUNK * c + CHUNK].reshape(n, depth)
+        tail_acc[...] = jnp.zeros_like(tail_acc)
+        for c in range(0, chunks, WIDE):
+            nk = CHUNK * (c + WIDE)
             k = bkv[0, g, :nk]
-            dk, dv, ds = piece(k, bkv[1, g, :nk], q, do, lse, delta, mask)
+            dk, dv, ds = piece(k, bkv[1, g, :nk], g, c, WIDE, mask)
             tail_acc[0, :nk] += dk
             tail_acc[1, :nk] += dv
-            dq_acc[g, c] = lax.dot_general(k, ds, (((0,), (0,)), ((), ())), preferred_element_type=F32)
-        if last < chunks:
-            return
+            dq = lax.dot_general(k, ds, (((0,), (0,)), ((), ())), preferred_element_type=F32)
+            dq_acc[g, :, places(c, WIDE)[1]] = dq
         bout[0, pl.ds(g, seq, stride=groups), :] = tail_acc[0] * scale
         bout[1, pl.ds(g, seq, stride=groups), :] = tail_acc[1]
 
-    def prompt_chunks(g, first, last):
-        k = kv[0, g].reshape(prompt, depth)
-        v = kv[1, g].reshape(prompt, depth)
-        for c in range(first, last):
-            q = q_s[g, CHUNK * c : CHUNK * c + CHUNK].reshape(n, depth)
-            do = do_s[g, CHUNK * c : CHUNK * c + CHUNK].reshape(n, depth)
-            dk, dv, ds = piece(k, v, q, do, rows_s[0, g, c], rows_s[1, g, c], None)
-            ds_s[g, c] = ds
+    def prompt_chunks(g, low, high, first, last):
+        rows = slice(32 * low, 32 * high)
+        k = kv[0, g, low:high].reshape(32 * (high - low), depth)
+        v = kv[1, g, low:high].reshape(32 * (high - low), depth)
+        wide = ALL // (high - low)
+        for c in range(first, last, wide):
+            dk, dv, ds = piece(k, v, g, c, wide, None)
+            ds_s[g, rows, places(c, wide)[1]] = ds
             if c:
-                acc[0] += dk
-                acc[1] += dv
+                acc[g, 0, rows] += dk
+                acc[g, 1, rows] += dv
             else:
-                acc[0] = dk
-                acc[1] = dv
+                acc[g, 0, rows] = dk
+                acc[g, 1, rows] = dv
 
     def query_part(g):
         k = kv[0, g].reshape(prompt, depth)
-        for c in range(chunks):
-            dq = lax.dot_general(k, ds_s[g, c], (((0,), (0,)), ((), ())), preferred_element_type=F32)
-            dq = ((dq + dq_acc[g, c]) * scale).T.astype(BF16)
-            dq_s[g, CHUNK * c : CHUNK * c + CHUNK] = dq.reshape(CHUNK, heads, depth)
+        for c in range(0, chunks, QWIDE):
+            at, lanes = places(c, QWIDE)
+            dq = lax.dot_general(k, ds_s[g, :, lanes], (((0,), (0,)), ((), ())), preferred_element_type=F32)
+            dq = ((dq + dq_acc[g, :, lanes]) * scale).T.astype(BF16)
+            dq_s[g, at] = dq.reshape(CHUNK * QWIDE, heads, depth)
 
     def line_done():
         whole = remote(line.at[:7], line.at[:7], line_sem.at[0], line_sem.at[1], sibling, h)
@@ -175,79 +197,120 @@
         whole.wait_send()
         line_f[...] = line[...].reshape(8 * 32, depth).astype(F32)
         for g in range(groups):
-            kv[core, g, plane] = line_f[pl.ds(h * groups + g, 32, stride=2 * groups), :].astype(BF16)
-
-    def plane_send(g):
-        block = kv.at[core, g, plane]
-        for step in PLANE:
-            remote(block, block, plane_sem.at[0, g], plane_sem.at[1, g], plane_peer(step)[1], h).start()
+            kv[core, g, 0] = line_f[pl.ds(h * groups + g, 32, stride=2 * groups), :].astype(BF16)
+
+    def plane_send(g, low, high):
+        for slot in reversed(range(max(low, 1), high)):
+            dst = kv.at[core, g, back(slot)]
+            remote(kv.at[core, g, 0], dst, plane_sem.at[0, g], plane_sem.at[1, g], plane_peer(slot), h).start()
+
+    def near_send(g):
+        mine = kv.at[core, g, 0]
+        for slot in reversed(range(1, NEAR)):
+            for on in (core, 1 - core):
+                dst = kv.at[core, g, back(slot)]
+                remote(mine, dst, near_sem.at[0, g], near_sem.at[1, g], plane_peer(slot, on), h).start()
+        remote(mine, mine, near_sem.at[0, g], near_sem.at[1, g], sibling, h).start()
+
+    def near_copies(g):
+        return remote(kv.at[0, g, :15], kv.at[0, g, :15], near_sem.at[0, g], near_sem.at[1, g], sibling, h)
+
+    def near_wait(g):
+        near_copies(g).wait_recv()
+
+    def plane_copies(g):
+        blocks = kv.at[core, g, : ALL - NEAR if g < SPLIT else 15]
+        return remote(blocks, blocks, plane_sem.at[0, g], plane_sem.at[1, g], sibling, h)
+
+    def fwd_copy(g, kind):
+        blocks = kv.at[kind, g, NEAR if g < SPLIT else 0 :]
+        return remote(blocks, blocks, fwd_sem.at[0, g], fwd_sem.at[1, g], sibling, h)
 
     def forward(g):
-        blocks = kv.at[core, g, :15]
-        remote(blocks, blocks, plane_sem.at[0, g], plane_sem.at[1, g], sibling, h).wait_recv()
-        remote(kv.at[core, g], kv.at[core, g], fwd_sem.at[0, g], fwd_sem.at[1, g], sibling, h).start()
+        plane_copies(g).wait_recv()
+        fwd_copy(g, core).start()
 
     def forwarded(g):
-        remote(kv.at[1 - core, g], kv.at[1 - core, g], fwd_sem.at[0, g], fwd_sem.at[1, g], sibling, h).wait_recv()
-
-    def pair_copy(g):
-        return remote(half.at[g, 1 - core], half_in.at[g], pair_sem.at[0, g], pair_sem.at[1, g], sibling, h)
-
-    def pair_start(g):
-        half[g, 0] = (acc[0] * scale).astype(BF16)
-        half[g, 1] = acc[1].astype(BF16)
-        pair[g] = acc[core] * jnp.where(core == 0, scale, 1.0)
-        pair_copy(g).start()
-
-    def plane_start(g):
-        pair_copy(g).wait_recv()
-        total = pair[g] + half_in[g].astype(F32)
-        spot[g] = total.astype(BF16).reshape(16, 32, depth)
-        for step in PLANE:
-            to, pb = plane_peer(step)
-            remote(spot.at[g, to], spot_in.at[g, plane], red_sem.at[0, g], red_sem.at[1, g], pb, h).start()
-        spot_in[g, plane] = spot[g, plane]
+        fwd_copy(g, 1 - core).wait_recv()
+
+    def pair_copy(u):
+        g, low, high = UNITS[u]
+        rows = pl.ds(32 * low, 32 * (high - low))
+        return remote(half.at[g, 1 - core, rows], half_in.at[g, rows], pair_sem.at[0, u], pair_sem.at[1, u], sibling, h)
+
+    def pair_start(u):
+        g, low, high = UNITS[u]
+        rows = slice(32 * low, 32 * high)
+        half[g, 0, rows] = (acc[g, 0, rows] * scale).astype(BF16)
+        half[g, 1, rows] = acc[g, 1, rows].astype(BF16)
+        pair[g, rows] = acc[g, core, rows] * jnp.where(core == 0, scale, 1.0)
+        pair_copy(u).start()
+
+    def plane_start(u):
+        g, low, high = UNITS[u]
+        rows = slice(32 * low, 32 * high)
+        pair_copy(u).wait_recv()
+        total = pair[g, rows] + half_in[g, rows].astype(F32)
+        spot[g, low:high] = total.astype(BF16).reshape(high - low, 32, depth)
+        for slot in reversed(range(max(low, 1), high)):
+            remote(spot.at[g, slot], spot_in.at[g, slot], red_sem.at[0, u], red_sem.at[1, u], plane_peer(slot), h).start()
+        if low == 0:
+            spot_in[g, 0] = spot[g, 0]
+
+    def red_copies(u):
+        g, low, high = UNITS[u]
+        blocks = spot_in.at[g, : high - max(low, 1)]
+        return remote(blocks, blocks, red_sem.at[0, u], red_sem.at[1, u], sibling, h)
 
     def plane_done(g):
-        blocks = spot_in.at[g, :15]
-        remote(blocks, blocks, red_sem.at[0, g], red_sem.at[1, g], sibling, h).wait_recv()
+        for u, unit in enumerate(UNITS):
+            if unit[0] == g:
+                red_copies(u).wait_recv()
         owned[...] = jnp.sum(spot_in[g].astype(F32), axis=0)
         for o in range(8):
             fin[o, 4 * g : 4 * g + 4] = owned[4 * o : 4 * o + 4]
 
-    suffix(0, 0, chunks)
-    suffix(1, 0, chunks // 2)
+    suffix(0)
+    suffix(1)
     line_done()
-    plane_send(0)
-    plane_send(1)
-    suffix(1, chunks // 2, chunks)
-    suffix(2, 0, chunks)
-    suffix(3, 0, chunks // 2)
-    forward(0)
-    plane_send(2)
-    plane_send(3)
-    suffix(3, chunks // 2, chunks)
+    for g in range(SPLIT):
+        near_send(g)
+        plane_send(g, NEAR, ALL)
+    suffix(2)
+    plane_send(2, 0, ALL)
+    suffix(3)
     for i in range(2):
         fin_b[i] = bout[i].astype(BF16)
+    near_wait(0)
+    prompt_chunks(0, 0, NEAR, 0, chunks)
+    forward(0)
+    plane_send(3, 0, ALL)
+    near_wait(1)
+    prompt_chunks(1, 0, NEAR, 0, chunks)
+    forward(1)
     forwarded(0)
-    prompt_chunks(0, 0, chunks // 2)
-    forward(1)
-    prompt_chunks(0, chunks // 2, chunks)
+    prompt_chunks(0, NEAR, ALL, 0, chunks)
     pair_start(0)
-    for g in range(1, groups):
-        forwarded(g)
-        if g == 1:
-            prompt_chunks(g, 0, chunks // 2)
-            forward(g + 1)
-            prompt_chunks(g, chunks // 2, chunks)
-        else:
-            if g + 1 < groups:
-                forward(g + 1)
-            prompt_chunks(g, 0, chunks)
-        pair_start(g)
-        plane_start(g - 1)
+    forward(2)
+    forwarded(1)
+    prompt_chunks(1, NEAR, ALL, 0, chunks)
+    pair_start(1)
+    plane_start(0)
+    forwarded(2)
+    prompt_chunks(2, 0, ALL, 0, chunks // 2)
+    forward(3)
+    prompt_chunks(2, 0, ALL, chunks // 2, chunks)
+    pair_start(2)
+    plane_start(1)
+    forwarded(3)
+    prompt_chunks(3, NEAR, ALL, 0, chunks)
+    pair_start(3)
+    plane_start(2)
+    prompt_chunks(3, 0, NEAR, 0, chunks)
+    pair_start(4)
+    plane_start(3)
     query_part(0)
-    plane_start(groups - 1)
+    plane_start(4)
     for g in range(1, groups):
         query_part(g)
     for g in range(groups):
@@ -258,16 +321,17 @@
         other, pb, ph = line_peer(d)
         remote(owner_out.at[other], owner_in.at[place], own_sem.at[0], own_sem.at[1], pb, ph).start()
     owner_in[place] = owner_out[place]
+    for g in range(groups):
+        if g < SPLIT:
+            near_copies(g).wait_send()
+        plane_copies(g).wait_send()
+        fwd_copy(g, core).wait_send()
+    for u in range(len(UNITS)):
+        pair_copy(u).wait_send()
+        red_copies(u).wait_send()
     whole = remote(owner_in.at[:7], owner_in.at[:7], own_sem.at[0], own_sem.at[1], sibling, h)
     whole.wait_recv()
     whole.wait_send()
-    for g in range(groups):
-        blocks = spot.at[g, :15]
-        remote(blocks, blocks, red_sem.at[0, g], red_sem.at[1, g], sibling, h).wait_send()
-        pair_copy(g).wait_send()
-        blocks = kv.at[core, g, :15]
-        remote(blocks, blocks, plane_sem.at[0, g], plane_sem.at[1, g], sibling, h).wait_send()
-        remote(kv.at[core, g], kv.at[core, g], fwd_sem.at[0, g], fwd_sem.at[1, g], sibling, h).wait_send()
 
 
 def write_out(dq_s, branch_s, owner_in, dq_hbm, dbk_hbm, dbv_hbm, dpk_hbm, dpv_hbm, owned, rows, rows_b, sems):
@@ -317,11 +381,12 @@
         scratch_shapes=[
             vm((groups, seq, heads, depth), BF16),
             vm((groups, seq, heads, depth), BF16),
-            vm((groups, seq // CHUNK, depth, CHUNK * heads), F32),
-            vm((groups, seq // CHUNK, prompt, CHUNK * heads), BF16),
+            vm((2, groups, depth, seq * heads), BF16),
+            vm((groups, depth, seq * heads), F32),
+            vm((groups, prompt, seq * heads), BF16),
             vm((head_count, seq), F32),
             vm((head_count, seq), F32),
-            vm((2, groups, seq // CHUNK, 1, CHUNK * heads), F32),
+            vm((2, groups, 1, seq * heads), F32),
             vm((2, own * all_groups, depth), BF16),
             vm((2, seq * groups, depth), BF16),
             vm((2, groups, seq, depth), BF16),
@@ -329,7 +394,7 @@
             vm((2, groups, 16, prompt // 16, depth), BF16),
             vm((8, own * all_groups, depth), BF16),
             vm((8 * own * all_groups, depth), F32),
-            vm((2, prompt, depth), F32),
+            vm((groups, 2, prompt, depth), F32),
             vm((2, seq, depth), F32),
             vm((groups, prompt, depth), F32),
             vm((groups, 2, prompt, depth), BF16),
@@ -341,8 +406,8 @@
             vm((8, groups * own, depth), F32),
             vm((2, seq * groups, depth), F32),
             pltpu.SMEM((1,), jnp.int32),
-            sem((7,)), sem((2, groups)), sem((2,)), sem((2, groups)),
-            sem((2, groups)), sem((2, groups)), sem((2, groups)), sem((2,)),
+            sem((7,)), sem((2, groups)), sem((2,)), sem((2, SPLIT)), sem((2, groups)),
+            sem((2, groups)), sem((2, len(UNITS))), sem((2, len(UNITS))), sem((2,)),
         ],
         compiler_params=pltpu.CompilerParams(
             collective_id=0, has_side_effects=True, vmem_limit_bytes=48 * 1024 * 1024

time: 42.4 us -> 41.1 us (0.969)
  Pallas kernels: 40.9 us -> 39.6 us
    pallas_call x1, Pallas kernels: 39.3 us -> 38 us  [shards(): pl.pallas_call(body, out_shape=[vm((groups, seq, heads, depth), BF16), vm...]
where the time goes in v3:
time: 41.1 us; the launch traced here: 41 us
  Pallas kernels  39.6 us (96%)
  between operations  1.45 us (4%)
    pallas_call x1, Pallas kernels, shards(): pl.pallas_call(body, out_shape=[vm((groups, seq, heads, depth), BF16), vm...  38 us
    pallas_call x1, Pallas kernels, shards(): pl.pallas_call(write_out, out_shape=[jax.ShapeDtypeStruct((seq, groups, h...  1.56 us

profile of v3, /device:TPU:1, one launch (start us, length us, event | category | flops | bytes accessed | tf_op | source)
XLA Modules:
  0.0 41.0 jit_solution(6052939977820645453)
XLA Ops:
  1.3 38.0 %shard_map.128 = (bf16[4,256,8,128]{3,2,1,0:T(8,128)(2,1)S(1)}, bf16[2,1024,128]{2,1,0:T(8,128)(2,1)S(1)}, bf16[8,16,128]{2,1,0:T(8,128)(2,1)S(1)}) custom-call(s32[1]{0:T(128)S(6)} %copy.14.refs_0_, bf16[256,4,8,128]{3,2,1,0:T(8,128)(2,1)} %bitcast.13, bf16[256,4,8,128]{3,2,1,0:T(8,128)(2,1)} %bitcast.14, f32[32,256]{1,0:T(8,128)} %bitcast.17, ...), custom_call_target="tpu_custom_call" | custom-call | tf_op jit(solution)/shard_map/pallas_call | solution.py:372
  39.3 1.6 %shard_map.129 = (bf16[256,4,8,128]{3,2,1,0:T(8,128)(2,1)}, bf16[1024,128]{1,0:T(8,128)(2,1)}, bf16[1024,128]{1,0:T(8,128)(2,1)}, bf16[32,128]{1,0:T(8,128)(2,1)}, bf16[32,128]{1,0:T(8,128)(2,1)}) custom-call(bf16[4,256,8,128]{3,2,1,0:T(8,128)(2,1)S(1)} %get-tuple-element.13.dq_s, bf16[2,1024,128]{2,1,0:T(8,128)(2,1)S(1)} %get-tuple-element.14.branch_s, ...), custom_call_target="tpu_custom_call" | custom-call | tf_op jit(solution)/shard_map/pallas_call | solution.py:431

commit v4 on v3

--- a/solution.py
+++ b/solution.py
@@ -277,15 +277,15 @@
         near_send(g)
         plane_send(g, NEAR, ALL)
     suffix(2)
-    plane_send(2, 0, ALL)
     suffix(3)
     for i in range(2):
         fin_b[i] = bout[i].astype(BF16)
     near_wait(0)
+    plane_send(2, 0, ALL)
     prompt_chunks(0, 0, NEAR, 0, chunks)
     forward(0)
+    near_wait(1)
     plane_send(3, 0, ALL)
-    near_wait(1)
     prompt_chunks(1, 0, NEAR, 0, chunks)
     forward(1)
     forwarded(0)

time: 41.1 us -> 40.9 us (level)
  no operation moved by 1% of the time
where the time goes in v4:
time: 40.9 us; the launch traced here: 40.8 us
  Pallas kernels  39.3 us (96%)
  between operations  1.45 us (4%)
    pallas_call x1, Pallas kernels, shards(): pl.pallas_call(body, out_shape=[vm((groups, seq, heads, depth), BF16), vm...  37.7 us
    pallas_call x1, Pallas kernels, shards(): pl.pallas_call(write_out, out_shape=[jax.ShapeDtypeStruct((seq, groups, h...  1.56 us

profile of v4, /device:TPU:1, one launch (start us, length us, event | category | flops | bytes accessed | tf_op | source)
XLA Modules:
  0.0 40.8 jit_solution(13902337836829809231)
XLA Ops:
  1.3 37.7 %shard_map.128 = (bf16[4,256,8,128]{3,2,1,0:T(8,128)(2,1)S(1)}, bf16[2,1024,128]{2,1,0:T(8,128)(2,1)S(1)}, bf16[8,16,128]{2,1,0:T(8,128)(2,1)S(1)}) custom-call(s32[1]{0:T(128)S(6)} %copy.14.refs_0_, bf16[256,4,8,128]{3,2,1,0:T(8,128)(2,1)} %bitcast.13, bf16[256,4,8,128]{3,2,1,0:T(8,128)(2,1)} %bitcast.14, f32[32,256]{1,0:T(8,128)} %bitcast.17, ...), custom_call_target="tpu_custom_call" | custom-call | tf_op jit(solution)/shard_map/pallas_call | solution.py:372
  39.0 1.6 %shard_map.129 = (bf16[256,4,8,128]{3,2,1,0:T(8,128)(2,1)}, bf16[1024,128]{1,0:T(8,128)(2,1)}, bf16[1024,128]{1,0:T(8,128)(2,1)}, bf16[32,128]{1,0:T(8,128)(2,1)}, bf16[32,128]{1,0:T(8,128)(2,1)}) custom-call(bf16[4,256,8,128]{3,2,1,0:T(8,128)(2,1)S(1)} %get-tuple-element.13.dq_s, bf16[2,1024,128]{2,1,0:T(8,128)(2,1)S(1)} %get-tuple-element.14.branch_s, ...), custom_call_target="tpu_custom_call" | custom-call | tf_op jit(solution)/shard_map/pallas_call | solution.py:431
